TPU v7x, 512 devices: a whole 4x8x8 slice. The times are simulated.
512 devices in a mesh: lat: 64 (over y, z), ma: 8 (over x, core).
Axes of the slice: x: 4, y: 8, z: 8, core: 2. Of those that a mesh axis runs over, the one named last changes fastest.
Arguments:
- pair_wave: int32 [360], replicated, may hold values from 0 to 359, each once
- legendre: bfloat16 [360, 640, 768], P('ma', 'lat'), may hold values from -0.0078125 to 0.0078125
- coefs: bfloat16 [360, 768, 168], P('ma', 'lat'), may hold values from -6 to 6
Outputs:
- noise: float32 [53760, 1440], P(('lat', 'ma'))
Inputs may be any that keep to these rules, and one draw needn't show every extreme that they name: Slot q holds wavenumbers pair_wave[q] and 719 - pair_wave[q]; every value appears once.
All inputs are finite; a program needn't handle non-finite values.
Results may differ from a plain program's by a relative error of at most 0.0003.
Values may be sent and summed in bfloat16 or wider, within the bound.
A program may use at most 64 MiB of HBM per device.

v0:
```python
import math

import jax
import jax.numpy as jnp
from jax import lax
from jax.sharding import Mesh
from jax.sharding import PartitionSpec as P

DEG = 720
LON = 1440
CH = 84
LAT_DEV = 10
MA = ("ma_0", "ma_1")
LAT_MA = ("lat", "ma_0", "ma_1")


def split_up(shard, dim, count):
    before, after = (shard.shape[:dim], shard.shape[dim + 1 :])
    return jnp.moveaxis(shard.reshape(*before, count, -1, *after), dim, 0)


def in_order(pieces, dim):
    pieces = jnp.moveaxis(pieces, 0, dim)
    dims = pieces.shape
    return pieces.reshape(*dims[:dim], dims[dim] * dims[dim + 1], *dims[dim + 2 :])


def moved_by_axis(pieces, axes, turns):
    dims = [lax.axis_size(a) for a in axes]
    pieces = pieces.reshape(*dims, *pieces.shape[1:])
    for k in turns:
        pieces = lax.all_to_all(pieces, axes[k], split_axis=k, concat_axis=k, tiled=True)
    return pieces.reshape(-1, *pieces.shape[len(axes) :])


def exchange_by_axis(shard, axes, turns, split_dim, concat_dim):
    pieces = split_up(shard, split_dim, lax.axis_size(axes))
    return in_order(moved_by_axis(pieces, axes, turns), concat_dim)


def chain_table(table, wave_ids, degree_top):
    row_count = table.shape[2]
    row_ids = jnp.arange(row_count, dtype=jnp.int32)[None, :]
    split_row = (degree_top - wave_ids)[:, None]
    inside = row_ids < split_row
    outside = (row_ids >= split_row) & (row_ids <= degree_top)
    masks = jnp.stack([inside, outside], axis=1)
    return jnp.where(masks[:, :, None, :], table[:, None, :, :], jnp.zeros((), table.dtype))


def fourier_basis(pair_wave, degree_top, lon_count):
    orders = jnp.stack([pair_wave, degree_top - 1 - pair_wave], axis=1)
    positions = jnp.arange(lon_count, dtype=jnp.int32)
    phase_int = orders[:, :, None] * positions[None, None, :] % lon_count
    radians = 2.0 * math.pi / lon_count * phase_int.astype(jnp.float32)
    weight = jnp.where(orders == 0, 1.0, 2.0).astype(jnp.float32)[:, :, None]
    real_row = weight * jnp.cos(radians)
    imag_row = -weight * jnp.sin(radians)
    return jnp.stack([real_row, imag_row], axis=2).reshape(-1, lon_count)


def body(pair_wave, legendre, coefs):
    lat_count = lax.axis_size("lat")
    lat_place = lax.axis_index("lat")
    ma_place = lax.axis_index(MA)
    slot_count = coefs.shape[0]
    wave_ids = lax.dynamic_slice_in_dim(pair_wave, ma_place * slot_count, slot_count)
    per_device = (slot_count + lat_count - 1) // lat_count
    extra = per_device * lat_count - slot_count
    table_pad = jnp.concatenate(
        [legendre, jnp.zeros((extra,) + legendre.shape[1:], legendre.dtype)], axis=0
    )
    coefs_pad = jnp.concatenate([coefs, jnp.zeros((extra,) + coefs.shape[1:], coefs.dtype)], axis=0)
    waves_pad = jnp.concatenate([wave_ids, jnp.zeros((extra,), jnp.int32)], axis=0)
    tables_in, coefs_in = (
        lax.all_to_all(table_pad, "lat", split_axis=0, concat_axis=1, tiled=True),
        lax.all_to_all(coefs_pad, "lat", split_axis=0, concat_axis=1, tiled=True),
    )
    my_waves = lax.dynamic_slice_in_dim(waves_pad, lat_place * per_device, per_device)
    masked = chain_table(tables_in, my_waves, DEG)
    sums = jnp.einsum("qeir,qrc->qeic", masked, coefs_in, preferred_element_type=jnp.float32)
    returned = lax.all_to_all(sums, "lat", split_axis=2, concat_axis=0, tiled=True)
    spectra = returned[:slot_count]
    arranged = jnp.transpose(
        spectra.reshape(slot_count, 2, LAT_DEV, 2, CH), (0, 1, 3, 2, 4)
    ).reshape(slot_count, 2, 2, LAT_DEV * CH)
    exchanged = exchange_by_axis(arranged, MA, (1, 0), 3, 0)
    fourier_rows = exchanged.reshape(-1, exchanged.shape[3])
    synth_basis = fourier_basis(pair_wave, DEG, LON)
    return lax.dot_general(
        fourier_rows, synth_basis, (((0,), (0,)), ((), ())), precision=lax.Precision.HIGHEST
    )


def solution(mesh):
    split = Mesh(mesh.devices.reshape(mesh.shape["lat"], 4, 2), ("lat", "ma_0", "ma_1"))
    placed = (P(), P(MA, "lat", None), P(MA, "lat", None))
    return jax.shard_map(
        body, mesh=split, in_specs=placed, out_specs=P(LAT_MA, None), check_vma=False
    )
```

profile of v0, /device:TPU:1, one launch (start us, length us, event | category | flops | bytes accessed | tf_op | source)
XLA Modules:
  0.0 170.7 jit_solution(15079287082618436240)
XLA Ops:
  0.0 1.1 copy.42
  1.1 0.1 concatenate.18
  1.1 0.0 copy-start
  1.1 1.3 reshape.144
  2.4 17.1 %all-to-all-start.1 = ((bf16[64,2,1008]{2,1,0:T(2,128)(2,1)}), bf16[64,2,1008]{2,1,0:T(2,128)(2,1)S(1)}, u32[]{:S(2)}, u32[]{:S(2)}) async-start(bf16[64,2,1008]{2,1,0:T(2,128)(2,1)} %reshape.144), calls=%async_computation.1 | async-start | bytes 524288 | tf_op jit(solution)/shard_map/all_to_all | solution.py:77
  19.6 1.4 copy.41
  20.9 1.3 concatenate.17
  22.2 10.2 %all-to-all-done.1 = bf16[64,2,1008]{2,1,0:T(2,128)(2,1)S(1)} async-done(((bf16[64,2,1008]{2,1,0:T(2,128)(2,1)}), bf16[64,2,1008]{2,1,0:T(2,128)(2,1)S(1)}, u32[]{:S(2)}, u32[]{:S(2)}) %all-to-all-start.1) | async-done | bytes 258080 | tf_op jit(solution)/shard_map/all_to_all | solution.py:77
  32.4 5.6 %all-to-all-start = ((bf16[64,10,768]{2,1,0:T(8,128)(2,1)}), bf16[64,10,768]{2,1,0:T(8,128)(2,1)S(1)}, u32[]{:S(2)}, u32[]{:S(2)}) async-start(bf16[64,10,768]{2,1,0:T(8,128)(2,1)} %concatenate.17), calls=%async_computation | async-start | bytes 3145728 | tf_op jit(solution)/shard_map/all_to_all | solution.py:76
  38.1 0.0 copy-done
  38.1 0.1 dynamic_slice.6
  38.2 0.6 fusion.16
  38.7 0.7 compare_and_fusion
  39.4 0.7 reshape.145
  40.1 0.2 reshape.139
  40.3 34.3 %all-to-all-done = bf16[64,10,768]{2,1,0:T(8,128)(2,1)S(1)} async-done(((bf16[64,10,768]{2,1,0:T(8,128)(2,1)}), bf16[64,10,768]{2,1,0:T(8,128)(2,1)S(1)}, u32[]{:S(2)}, u32[]{:S(2)}) %all-to-all-start) | async-done | bytes 983072 | tf_op jit(solution)/shard_map/all_to_all | solution.py:76
  74.6 0.4 broadcast_in_dim.43
  75.0 0.8 fusion.8
  75.8 2.0 %copy.44 = f32[1,2,640,168]{3,1,0,2:T(2,128)} copy(f32[1,2,640,168]{2,3,1,0:T(8,128)S(1)} %fusion.8) | data formatting | bytes 1720320 | tf_op jit(solution)/shard_map/qeir,qrc->qeic/dot_general | solution.py:81
  77.9 10.3 %all-to-all-start.2 = ((f32[1,2,640,168]{3,1,0,2:T(2,128)}), f32[1,2,640,168]{3,1,0,2:T(2,128)S(1)}, u32[]{:S(2)}, u32[]{:S(2)}) async-start(f32[1,2,640,168]{3,1,0,2:T(2,128)} %copy.44), calls=%async_computation.2 | async-start | bytes 2621440 | tf_op jit(solution)/shard_map/all_to_all | solution.py:82
  88.3 21.3 %cosine_multiply_fusion = (f32[360,2,1,1440]{3,0,2,1:T(8,128)}, f32[360,2,1,1440]{3,0,2,1:T(8,128)}) fusion(s32[360,2]{0,1:T(2,128)S(1)} %pad_add_fusion, f32[360,2]{0,1:T(2,128)S(1)} %get-tuple-element.7, f32[360,2]{0,1:T(2,128)S(1)} %get-tuple-element.8), kind=kLoop, calls=%fused_computation.5 | loop fusion | flops 11404800 | bytes 8303040 | tf_op jit(solution)/shard_map/mul | solution.py:57
  109.6 9.3 %all-to-all-done.2 = f32[1,2,640,168]{3,1,0,2:T(2,128)S(1)} async-done(((f32[1,2,640,168]{3,1,0,2:T(2,128)}), f32[1,2,640,168]{3,1,0,2:T(2,128)S(1)}, u32[]{:S(2)}, u32[]{:S(2)}) %all-to-all-start.2) | async-done | bytes 860192 | tf_op jit(solution)/shard_map/all_to_all | solution.py:82
  118.9 0.3 slice.5
  119.2 1.2 reshape.140
  120.4 0.2 copy.52
  120.6 0.6 reshape_reshape.3
  121.2 0.4 copy.46
  121.6 9.1 %all_to_all.43 = f32[4,2,45,2,2,105]{5,4,3,2,0,1:T(2,128)S(1)} all-to-all(f32[4,2,45,2,2,105]{5,4,3,2,0,1:T(2,128)S(1)} %copy.46), channel_id=1, replica_groups=mesh['lat'=64,'ma_0'=4,'ma_1'=2] {'ma_1'}, dimensions={1} | all-to-all | bytes 1209600 | tf_op jit(solution)/shard_map/all_to_all | solution.py:32
  130.7 1.2 copy.47
  131.9 4.0 %all-to-all-start.4 = ((f32[4,2,45,2,2,105]{5,4,3,2,1,0:T(2,128)}), f32[4,2,45,2,2,105]{5,4,3,2,1,0:T(2,128)S(1)}, u32[]{:S(2)}, u32[]{:S(2)}) async-start(f32[4,2,45,2,2,105]{5,4,3,2,1,0:T(2,128)} %copy.47), calls=%async_computation.4 | async-start | bytes 1474560 | tf_op jit(solution)/shard_map/all_to_all | solution.py:32
  135.9 4.4 %pad_maximum_fusion = f32[360,2,2,1440]{3,0,2,1:T(8,128)S(1)} fusion(f32[360,2,1,1440]{3,0,2,1:T(8,128)} %get-tuple-element.6, f32[360,2,1,1440]{3,0,2,1:T(8,128)} %get-tuple-element.5), kind=kLoop, calls=%fused_computation | loop fusion | flops 2073600 | bytes 16588800 | tf_op jit(solution)/shard_map/stack | solution.py:59
  140.3 10.9 %copy.48 = f32[360,2,2,1440]{3,2,1,0:T(2,128)} copy(f32[360,2,2,1440]{3,0,2,1:T(8,128)S(1)} %pad_maximum_fusion) | data formatting | bytes 16588800 | tf_op jit(solution)/shard_map/stack | solution.py:59
  151.2 11.4 %reshape.142 = f32[1440,1440]{1,0:T(8,128)} reshape(f32[360,2,2,1440]{3,2,1,0:T(2,128)} %copy.48) | data formatting | bytes 16588800 | tf_op jit(solution)/shard_map/reshape | solution.py:59
  162.6 0.0 all-to-all-done.4
  162.6 8.1 %fusion.17 = f32[105,1440]{1,0:T(8,128)} fusion(f32[1440,105]{1,0:T(8,128)S(1)} %bitcast.24, f32[1440,1440]{1,0:T(8,128)} %reshape.142), kind=kOutput, calls=%fused_computation.28 | convolution fusion | flops 2612736000 | bytes 9504000 | tf_op jit(solution)/shard_map/dot_general | solution.py:90
  (6 shorter events, 0.0 us)
Async XLA Ops:
  1.1 36.9 %copy-start = (s32[360]{0:T(512)S(1)}, s32[360]{0:T(512)}, u32[]{:S(2)}) copy-start(s32[360]{0:T(512)} %param.3) | copy-start | bytes 4324
  2.4 30.0 %all-to-all-start.1 = ((bf16[64,2,1008]{2,1,0:T(2,128)(2,1)}), bf16[64,2,1008]{2,1,0:T(2,128)(2,1)S(1)}, u32[]{:S(2)}, u32[]{:S(2)}) async-start(bf16[64,2,1008]{2,1,0:T(2,128)(2,1)} %reshape.144), calls=%async_computation.1 | async-start | bytes 524288 | tf_op jit(solution)/shard_map/all_to_all | solution.py:77
  32.4 42.2 %all-to-all-start = ((bf16[64,10,768]{2,1,0:T(8,128)(2,1)}), bf16[64,10,768]{2,1,0:T(8,128)(2,1)S(1)}, u32[]{:S(2)}, u32[]{:S(2)}) async-start(bf16[64,10,768]{2,1,0:T(8,128)(2,1)} %concatenate.17), calls=%async_computation | async-start | bytes 3145728 | tf_op jit(solution)/shard_map/all_to_all | solution.py:76
  77.9 41.0 %all-to-all-start.2 = ((f32[1,2,640,168]{3,1,0,2:T(2,128)}), f32[1,2,640,168]{3,1,0,2:T(2,128)S(1)}, u32[]{:S(2)}, u32[]{:S(2)}) async-start(f32[1,2,640,168]{3,1,0,2:T(2,128)} %copy.44), calls=%async_computation.2 | async-start | bytes 2621440 | tf_op jit(solution)/shard_map/all_to_all | solution.py:82
  131.9 30.7 %all-to-all-start.4 = ((f32[4,2,45,2,2,105]{5,4,3,2,1,0:T(2,128)}), f32[4,2,45,2,2,105]{5,4,3,2,1,0:T(2,128)S(1)}, u32[]{:S(2)}, u32[]{:S(2)}) async-start(f32[4,2,45,2,2,105]{5,4,3,2,1,0:T(2,128)} %copy.47), calls=%async_computation.4 | async-start | bytes 1474560 | tf_op jit(solution)/shard_map/all_to_all | solution.py:32
where the time goes:
time: 172 us; the launch traced here: 171 us
  waiting for transfers between devices  53.9 us (31%)
  starting transfers between devices  37.1 us (22%)
  local copies, waits for them, and re-layouts  34.5 us (20%)
  other arithmetic  27 us (16%)
  blocking collectives  9.12 us (5%)
  matrix products  8.94 us (5%)
    all_to_all x1, waiting for transfers between devices, body(): lax.all_to_all(table_pad, 'lat', split_axis=0, concat_axis=1, tiled=True)  34.3 us
    mul x1, other arithmetic, fourier_basis(): real_row = weight * jnp.cos(radians)  21.3 us
    all_to_all x1, starting transfers between devices, body(): lax.all_to_all(coefs_pad, 'lat', split_axis=0, concat_axis=1, tiled=True)  17.1 us
    reshape x1, local copies, waits for them, and re-layouts, fourier_basis(): return jnp.stack([real_row, imag_row], axis=2).reshape(-1, lon_count)  11.4 us
    another operation x1, local copies, waits for them, and re-layouts, fourier_basis(): return jnp.stack([real_row, imag_row], axis=2).reshape(-1, lon_count)  10.9 us
    all_to_all x1, starting transfers between devices, body(): lax.all_to_all(sums, 'lat', split_axis=2, concat_axis=0, tiled=True)  10.3 us
    all_to_all x1, waiting for transfers between devices, body(): lax.all_to_all(coefs_pad, 'lat', split_axis=0, concat_axis=1, tiled=True)  10.2 us
    all_to_all x1, waiting for transfers between devices, body(): lax.all_to_all(sums, 'lat', split_axis=2, concat_axis=0, tiled=True)  9.33 us
  transfers between devices with their start and end apart: 4, of which 3 were waited for; matrix products, arithmetic and copies ran while one was open for 31% of the time, Pallas kernels for 0%

commit v1 on v0

v1 whole, which is shorter than its diff:
```python
import math

import jax
import jax.numpy as jnp
import numpy as np
from jax import lax
from jax.experimental import pallas as pl
from jax.experimental.pallas import tpu as pltpu
from jax.sharding import Mesh
from jax.sharding import PartitionSpec as P

DEG = 720
LON = 1440
HALF = LON // 2
CH = 84
LAT = 10
SLOTS = 45
PER = 6
N = 8
ROWS = 105
RR = 768
F32 = jnp.float32
BF = jnp.bfloat16
MESH_ID = pl.DeviceIdType.MESH
FAR_FIRST = (4, 3, 5, 2, 6, 1, 7)
STRIDE = 88


def half_angle_fit():
    t = np.cos(np.linspace(0, np.pi, 4001)) * (np.pi / 2)
    sin_c = np.linalg.lstsq(np.stack([t ** (2 * i + 1) for i in range(5)], 1), np.sin(t), rcond=None)[0]
    cos_c = np.linalg.lstsq(np.stack([t ** (2 * i) for i in range(6)], 1), np.cos(t), rcond=None)[0]
    return [float(v) for v in sin_c], [float(v) for v in cos_c]


SIN_C, COS_C = half_angle_fit()


def horner(coefs, square):
    total = jnp.full_like(square, coefs[-1])
    for value in coefs[-2::-1]:
        total = total * square + value
    return total


def wave_rows(waves, weight, lon_at):
    product = waves * lon_at
    turns = jnp.round(product * (1.0 / LON))
    half = (product - turns * float(LON)) * (math.pi / LON)
    square = half * half
    sine = half * horner(SIN_C, square)
    cosine = horner(COS_C, square)
    twice = (2.0 * weight) * sine
    return weight - twice * sine, -twice * cosine


def split_bf16(x):
    high = x.astype(BF)
    return high, (x - high.astype(F32)).astype(BF)


def kernel(
    pw, leg_hbm, cf_hbm, out,
    leg, cf, cbuf, csend, crecv, gat, lbuf, lsend, lrecv, ltail, fbuf, fsend, frecv, fdec, ucol, bas,
    in_sem, own_sem, csem, lsem, fsem, ring_s, ring_r,
):
    y, z = lax.axis_index("y"), lax.axis_index("z")
    m = 2 * lax.axis_index("x") + lax.axis_index("c")

    def device(y_at, z_at, m_at):
        return (y_at, z_at, m_at // 2, m_at % 2)

    barrier = pltpu.get_barrier_semaphore()
    peers = [device((y + 1) % N, z, m), device((y + N - 1) % N, z, m)]
    peers += [device(y, (z + t) % N, m) for t in FAR_FIRST]
    peers += [device(y, z, (m + t) % N) for t in FAR_FIRST]
    for peer in peers:
        pl.semaphore_signal(barrier, inc=1, device_id=peer, device_id_type=MESH_ID)
    cf_in = pltpu.make_async_copy(cf_hbm, cf, in_sem.at[0])
    leg_in = pltpu.make_async_copy(leg_hbm, leg, in_sem.at[1])
    cf_in.start()
    leg_in.start()

    def slot_tile(ref, row, j):
        count = min(8, SLOTS - 8 * j)
        tile = ref[row, 8 * j : 8 * j + count, :].astype(F32)
        if count < 8:
            tile = jnp.concatenate([tile, jnp.zeros((8 - count, tile.shape[1]), F32)], 0)
        return tile

    cf_in.wait()
    for r in range(12):
        for g in range(2):
            tiles = [slot_tile(cf, r, 3 * g + k) for k in range(3)]
            at = 8 * (8 * r + 4 * g)
            for k in range(3):
                cbuf[at + 8 * k : at + 8 * k + 8, :] = tiles[k][:, :128]
            rest = [t[:, 128:] for t in tiles] + [jnp.zeros((8, 8), F32)]
            cbuf[at + 24 : at + 32, :] = jnp.concatenate(rest, 1)
    for d in range(N):
        csend[d] = cbuf[pl.ds(d, 96, stride=8), :].astype(BF)
    leg_in.wait()
    for i in range(LAT):
        for j in range(PER):
            at = 8 * (8 * j + i if i < 8 else 48 + 2 * j + i - 8)
            tile = slot_tile(leg, i, j)
            for l in range(6):
                lbuf[l, at : at + 8, :] = tile[:, 128 * l : 128 * l + 128]

    pl.semaphore_wait(barrier, len(peers))

    own_c = pltpu.make_async_copy(csend.at[z], crecv.at[z], own_sem.at[0])
    own_c.start()
    for t in FAR_FIRST:
        to = (z + t) % N
        pltpu.make_async_remote_copy(
            csend.at[to], crecv.at[z], csem.at[0], csem.at[1], device_id=device(y, to, m), device_id_type=MESH_ID
        ).start()

    def send_leg(to):
        pltpu.make_async_remote_copy(
            lsend.at[to], lrecv.at[z], lsem.at[0], lsem.at[1], device_id=device(y, to, m), device_id_type=MESH_ID
        ).start()

    for n, t in enumerate(FAR_FIRST + (0,)):
        to = (z + t) % N
        for l in range(6):
            lsend[to, :, 128 * l : 128 * l + 128] = lbuf[l, pl.ds(to, 60, stride=8), :].astype(BF)
        if n >= 1:
            send_leg((z + FAR_FIRST[n - 1]) % N)
    own_l = pltpu.make_async_copy(lsend.at[z], lrecv.at[z], own_sem.at[1])

    @pl.loop(0, PER * N)
    def _(tile):
        first = SLOTS * (tile % N) + 8 * (tile // N)
        rows = [jnp.full((1, 128), pw[jnp.minimum(first + d, 359)].astype(F32)) for d in range(8)]
        ucol[pl.ds(pl.multiple_of(tile * 8, 8), 8), :] = jnp.concatenate(rows, 0)

    own_l.start()
    lane = lax.broadcasted_iota(jnp.int32, (16, 128), 1).astype(F32)

    def make_basis(first, last):
        @pl.loop(first, last)
        def _(block):
            at = pl.multiple_of(block * 16, 16)
            u = ucol[pl.ds(at, 16), :]
            odd = u - 2.0 * jnp.floor(u * 0.5) > 0.5
            even_wave = jnp.where(odd, float(DEG - 1) - u, u)
            weight = jnp.where(even_wave == 0.0, 1.0, 2.0)
            for h, (wave, wt) in enumerate(((even_wave, weight), (float(DEG - 1) - even_wave, 2.0))):
                for l in range(6):
                    pair = wave_rows(wave, wt, lane + 128.0 * l)
                    for e in range(2):
                        high, low = split_bf16(pair[e])
                        to = pl.multiple_of(384 * e + at, 16)
                        bas[h, 0, pl.ds(to, 16), 128 * l : 128 * l + 128] = high
                        bas[h, 1, pl.ds(to, 16), 128 * l : 128 * l + 128] = low

    make_basis(0, 8)

    def wait_bytes(ref, sem):
        pltpu.make_async_copy(ref, ref, sem).wait()

    own_c.wait()
    wait_bytes(crecv.at[pl.ds(0, 7)], csem.at[1])
    for s in range(N):
        cbuf[96 * s : 96 * s + 96, :] = crecv[s].astype(F32)
    for blk in range(8):
        gat[y, blk] = cbuf[pl.ds(blk, 96, stride=8), :].astype(BF)

    def ring(way, step, half):
        origin = (y - step + N) % N if way == 0 else (y + step) % N
        part = gat.at[origin, pl.ds(4 * half, 4)]
        to = (y + 1) % N if way == 0 else (y + N - 1) % N
        return pltpu.make_async_remote_copy(
            part, part, ring_s.at[way, step, half], ring_r.at[way, step, half],
            device_id=device(to, z, m), device_id_type=MESH_ID,
        )

    for half in range(2):
        for way in range(2):
            ring(way, 0, half).start()
    done = 8
    for step in range(1, 4):
        for half in range(2):
            if done < 24:
                make_basis(done, min(done + 3, 24))
                done = min(done + 3, 24)
            for way in range(2):
                if step < 3 or way == half:
                    ring(way, step - 1, half).wait_recv()
                    ring(way, step, half).start()
    if done < 24:
        make_basis(done, 24)
    own_l.wait()
    wait_bytes(lrecv.at[pl.ds(0, 7)], lsem.at[1])
    for s in range(N):
        for l in range(6):
            ltail[l, 16 * s : 16 * s + 12, :] = lrecv[s, 48:60, 128 * l : 128 * l + 128].astype(F32)
    ring(0, 2, 1).wait_recv()
    ring(1, 2, 0).wait_recv()
    ring(0, 3, 0).wait_recv()
    ring(1, 3, 1).wait_recv()

    row_at = lax.broadcasted_iota(jnp.int32, (1, RR), 1)
    lane80 = lax.broadcasted_iota(jnp.int32, (80, 128), 1)
    for j in range(PER):
        u = pw[SLOTS * m + jnp.minimum(8 * j + z, SLOTS - 1)]
        cut = DEG - u
        odd = lax.rem(u, 2)
        low = (row_at < cut).astype(F32)
        high = (row_at <= DEG).astype(F32) - low
        swap = odd.astype(F32)
        masks = [(low + swap * (high - low)).astype(BF), (high + swap * (low - high)).astype(BF)]
        main = lrecv[:, 8 * j : 8 * j + 8, :].reshape(64, RR)
        tail = [[ltail[l, pl.ds(2 * j + k, 8, stride=16), :] for l in range(6)] for k in range(2)]
        tail = jnp.concatenate([jnp.concatenate(t, 1) for t in tail], 0)
        table = jnp.concatenate([main, tail.astype(BF)], 0)
        lhs = jnp.concatenate([table * masks[0], table * masks[1]], 0)
        g, k = divmod(j, 3)
        rhs = jnp.concatenate([gat[:, 4 * g + k].reshape(RR, 128), gat[:, 4 * g + 3].reshape(RR, 128)], 1)
        sums = jnp.dot(lhs, rhs, preferred_element_type=F32)
        for h in range(2):
            first = sums[80 * h : 80 * h + 80, :128]
            second = sums[80 * h : 80 * h + 80, 128:]
            imag = jnp.where(
                lane80 < 44, pltpu.roll(first, 44, axis=1), pltpu.roll(second, (44 - 40 * k) % 128, axis=1)
            )
            for e, value in enumerate((first, imag)):
                at = (12 * h + 6 * e + j) * STRIDE
                fbuf[at : at + 80, :] = value

    lane24 = lax.broadcasted_iota(jnp.int32, (24, 128), 1)

    def pack(to):
        lats = []
        for i in range(LAT):
            at = 8 * to + i if i < 8 else 64 + 8 * (i - 8) + to
            lats.append(fbuf[pl.ds(at, 24, stride=STRIDE), :])
        for k in range(N):
            i, skip = k + k // 4, 21 * (k % 4)
            keep = CH - skip
            first = pltpu.roll(lats[i], 128 - skip, axis=1) if skip else lats[i]
            window = jnp.where(lane24 < keep, first, pltpu.roll(lats[i + 1], keep, axis=1))
            window = jnp.where(lane24 < ROWS, window, 0.0)
            most = jnp.max(jnp.abs(window), axis=1, keepdims=True)
            level = jnp.ceil(jnp.log2(jnp.maximum(most, 1e-30)))
            scaled = jnp.clip(jnp.round(window * jnp.exp2(15.0 - level)), -32767.0, 32767.0)
            coded = jnp.where(lane24 < ROWS, scaled, jnp.broadcast_to(level, (24, 128)))
            fsend[to, k] = coded.astype(jnp.int32).astype(jnp.int16)

    def send_f(to):
        for t in range(N):
            m_to = (m + t) % N
            pltpu.make_async_remote_copy(
                fsend.at[to, m_to], frecv.at[m * N + z], fsem.at[0], fsem.at[1],
                device_id=device(y, to, m_to), device_id_type=MESH_ID,
            ).start()

    for n, t in enumerate(FAR_FIRST + (0,)):
        pack((z + t) % N)
        if n >= 1:
            send_f((z + FAR_FIRST[n - 1]) % N)
    for t in range(1, N):
        m_to = (m + t) % N
        pltpu.make_async_remote_copy(
            fsend.at[z, m_to], frecv.at[m * N + z], fsem.at[0], fsem.at[1],
            device_id=device(y, z, m_to), device_id_type=MESH_ID,
        ).start()
    own_f = pltpu.make_async_copy(fsend.at[z, m], frecv.at[m * N + z], own_sem.at[2])
    own_f.start()

    wait_bytes(csend.at[pl.ds(0, 7)], csem.at[0])
    wait_bytes(lsend.at[pl.ds(0, 7)], lsem.at[0])
    for way in range(2):
        for step in range(4):
            for half in range(2):
                if step < 3 or way == half:
                    ring(way, step, half).wait_send()
    own_f.wait()
    wait_bytes(frecv.at[pl.ds(0, 63)], fsem.at[1])

    lane192 = lax.broadcasted_iota(jnp.int32, (192, 128), 1)

    @pl.loop(0, 8)
    def _(part):
        coded = frecv[pl.ds(part * 8, 8)].astype(jnp.int32).astype(F32).reshape(192, 128)
        scale = jnp.exp2(coded[:, 127:128] - 15.0)
        fdec[pl.ds(pl.multiple_of(part * 192, 8), 192), :] = jnp.where(lane192 < ROWS, coded * scale, 0.0)

    lhs = []
    for h in range(2):
        rows = jnp.concatenate([fdec[pl.ds(12 * h + t, 64, stride=24), :] for t in range(12)], 0)
        high, low = split_bf16(jnp.transpose(rows))
        lhs.append((high, jnp.concatenate([high, low], 0)))
    for l in range(3):
        at = slice(256 * l, 256 * l + 256)
        part = []
        for h in range(2):
            high, both = lhs[h]
            wide = jnp.dot(both, bas[h, 0, :, at], preferred_element_type=F32)
            part.append(
                wide[:128] + wide[128:] + jnp.dot(high, bas[h, 1, :, at], preferred_element_type=F32)
            )
        count = min(256, HALF - 256 * l)
        out[:, 256 * l : 256 * l + count] = (part[0] + part[1])[:ROWS, :count]
        out[:, HALF + 256 * l : HALF + 256 * l + count] = (part[0] - part[1])[:ROWS, :count]
    wait_bytes(frecv.at[pl.ds(0, 63)], fsem.at[0])


def body(pair_wave, legendre, coefs):
    i16 = jnp.int16
    return pl.pallas_call(
        kernel,
        out_shape=jax.ShapeDtypeStruct((ROWS, LON), F32),
        in_specs=[
            pl.BlockSpec(memory_space=pltpu.SMEM),
            pl.BlockSpec(memory_space=pl.ANY),
            pl.BlockSpec(memory_space=pl.ANY),
        ],
        out_specs=pl.BlockSpec(memory_space=pltpu.VMEM),
        scratch_shapes=[
            pltpu.VMEM((LAT, SLOTS, RR), BF),
            pltpu.VMEM((12, SLOTS, 2 * CH), BF),
            pltpu.VMEM((768, 128), F32),
            pltpu.VMEM((N, 96, 128), BF),
            pltpu.VMEM((N, 96, 128), BF),
            pltpu.VMEM((N, 8, 96, 128), BF),
            pltpu.VMEM((6, 480, 128), F32),
            pltpu.VMEM((N, 60, RR), BF),
            pltpu.VMEM((N, 60, RR), BF),
            pltpu.VMEM((6, 128, 128), F32),
            pltpu.VMEM((24 * STRIDE, 128), F32),
            pltpu.VMEM((N, N, 24, 128), i16),
            pltpu.VMEM((N * N, 24, 128), i16),
            pltpu.VMEM((N * N * 24, 128), F32),
            pltpu.VMEM((384, 128), F32),
            pltpu.VMEM((2, 2, RR, RR), BF),
            pltpu.SemaphoreType.DMA((2,)),
            pltpu.SemaphoreType.DMA((3,)),
            pltpu.SemaphoreType.DMA((2,)),
            pltpu.SemaphoreType.DMA((2,)),
            pltpu.SemaphoreType.DMA((2,)),
            pltpu.SemaphoreType.DMA((2, 4, 2)),
            pltpu.SemaphoreType.DMA((2, 4, 2)),
        ],
        compiler_params=pltpu.CompilerParams(collective_id=0, has_side_effects=True, vmem_limit_bytes=40 << 20),
    )(pair_wave, jnp.transpose(legendre, (1, 0, 2)), jnp.transpose(coefs, (1, 0, 2)))


def solution(mesh):
    split = Mesh(mesh.devices.reshape(N, N, 4, 2), ("y", "z", "x", "c"))
    placed = (P(), P(("x", "c"), ("y", "z"), None), P(("x", "c"), ("y", "z"), None))
    return jax.shard_map(
        body, mesh=split, in_specs=placed, out_specs=P(("y", "z", "x", "c"), None), check_vma=False
    )
```

time: 172 us -> 62 us (0.36)
  Pallas kernels: 0 us -> 58.2 us
  waiting for transfers between devices: 53.9 us -> 0 us
  starting transfers between devices: 37.1 us -> 0 us
  local copies, waits for them, and re-layouts: 34.5 us -> 3.61 us
  other arithmetic: 27 us -> 0 us
  blocking collectives: 9.12 us -> 0 us
  matrix products: 8.94 us -> 0 us
    pallas_call x0 -> x1, Pallas kernels: none -> 58.2 us  [body(): pl.pallas_call(kernel, out_shape=jax.ShapeDtypeStruct((ROWS, LON), F32),...]
    all_to_all x4 -> x0, waiting for transfers between devices: 53.9 us -> none  [the longest x1 34.3 us: body(): lax.all_to_all(table_pad, 'lat', split_axis=0, concat_axis=1, tiled=True)]
    all_to_all x4 -> x0, starting transfers between devices: 37.1 us -> none  [the longest x1 17.1 us: body(): lax.all_to_all(coefs_pad, 'lat', split_axis=0, concat_axis=1, tiled=True)]
    mul x1 -> x0, other arithmetic: 21.3 us -> none  [fourier_basis(): real_row = weight * jnp.cos(radians)]
    reshape x4 -> x0, local copies, waits for them, and re-layouts: 13.1 us -> none  [the longest x1 11.4 us: fourier_basis(): return jnp.stack([real_row, imag_row], axis=2).reshape(-1, lon_count)]
    another operation x5 -> x0, local copies, waits for them, and re-layouts: 11.7 us -> none  [the longest x1 10.9 us: fourier_basis(): return jnp.stack([real_row, imag_row], axis=2).reshape(-1, lon_count)]
    all_to_all x1 -> x0, blocking collectives: 9.12 us -> none  [moved_by_axis(): lax.all_to_all(pieces, axes[k], split_axis=k, concat_axis=k, tiled=True)]
    dot_general x2 -> x0, matrix products: 8.94 us -> none  [the longest x1 8.11 us: body(): lax.dot_general(fourier_rows, synth_basis, (((0,), (0,)), ((), ())), prec...]
  transfers between devices with their start and end apart: 4 -> 0, of which waited for: 3 -> 0; matrix products, arithmetic and copies ran while one was open for 31% -> 0% of each run, Pallas kernels for 0% -> 0%
where the time goes in v1:
time: 62 us; the launch traced here: 61.8 us
  Pallas kernels  58.2 us (94%)
  local copies, waits for them, and re-layouts  3.61 us (6%)
    pallas_call x1, Pallas kernels, body(): pl.pallas_call(kernel, out_shape=jax.ShapeDtypeStruct((ROWS, LON), F32),...  58.2 us
    unnamed x7, local copies, waits for them, and re-layouts  3.61 us

profile of v1, /device:TPU:1, one launch (start us, length us, event | category | flops | bytes accessed | tf_op | source)
XLA Modules:
  0.0 61.8 jit_solution(15493956861128914787)
XLA Ops:
  0.0 0.0 copy-start.2
  0.0 0.7 %copy-done.2 = s32[360]{0:T(512)S(1)} copy-done((s32[360]{0:T(512)S(1)}, s32[360]{0:T(512)}, u32[]{:S(2)}) %copy-start.2) | copy-done | bytes 1464
  0.7 0.0 copy-start
  0.7 1.1 %copy-done = bf16[45,10,768]{2,0,1:T(8,128)(2,1)S(1)} copy-done((bf16[45,10,768]{2,0,1:T(8,128)(2,1)S(1)}, bf16[45,10,768]{2,0,1:T(8,128)(2,1)}, u32[]{:S(2)}) %copy-start) | copy-done | bytes 691224
  1.8 0.0 copy-start.1
  1.8 1.0 %copy-done.1 = bf16[45,12,168]{2,0,1:T(8,128)(2,1)S(1)} copy-done((bf16[45,12,168]{2,0,1:T(8,128)(2,1)S(1)}, bf16[45,12,168]{2,0,1:T(8,128)(2,1)}, u32[]{:S(2)}) %copy-start.1) | copy-done | bytes 181464
  2.8 58.2 %shard_map.37 = f32[105,1440]{1,0:T(8,128)S(1)} custom-call(s32[360]{0:T(512)S(1)} %copy-done.2, bf16[10,45,768]{2,1,0:T(8,128)(2,1)S(1)} %bitcast.2, bf16[12,45,168]{2,1,0:T(8,128)(2,1)S(1)} %bitcast.3), custom_call_target="tpu_custom_call" | custom-call | tf_op jit(solution)/shard_map/pallas_call | solution.py:313
  61.0 0.8 %copy.5 = f32[105,1440]{1,0:T(8,128)} copy(f32[105,1440]{1,0:T(8,128)S(1)} %shard_map.37) | data formatting | bytes 1209600
Async XLA Ops:
  0.0 0.7 %copy-start.2 = (s32[360]{0:T(512)S(1)}, s32[360]{0:T(512)}, u32[]{:S(2)}) copy-start(s32[360]{0:T(512)} %pw.1) | copy-start | bytes 4324
  0.7 1.1 %copy-start = (bf16[45,10,768]{2,0,1:T(8,128)(2,1)S(1)}, bf16[45,10,768]{2,0,1:T(8,128)(2,1)}, u32[]{:S(2)}) copy-start(bf16[45,10,768]{2,0,1:T(8,128)(2,1)} %param.4) | copy-start | bytes 2073604
  1.8 1.0 %copy-start.1 = (bf16[45,12,168]{2,0,1:T(8,128)(2,1)S(1)}, bf16[45,12,168]{2,0,1:T(8,128)(2,1)}, u32[]{:S(2)}) copy-start(bf16[45,12,168]{2,0,1:T(8,128)(2,1)} %param.5) | copy-start | bytes 544324

commit v2 on v1

--- a/solution.py
+++ b/solution.py
@@ -24,6 +24,8 @@
 MESH_ID = pl.DeviceIdType.MESH
 FAR_FIRST = (4, 3, 5, 2, 6, 1, 7)
 STRIDE = 88
+EARLY = 8
+SHRINK = 0.9999
 
 
 def half_angle_fit():
@@ -60,8 +62,8 @@
 
 
 def kernel(
-    pw, leg_hbm, cf_hbm, out,
-    leg, cf, cbuf, csend, crecv, gat, lbuf, lsend, lrecv, ltail, fbuf, fsend, frecv, fdec, ucol, bas,
+    pw_hbm, leg_hbm, cf_hbm, out,
+    pw, leg, cf, cbuf, csend, crecv, gat, lbuf, lsend, lrecv, ltail, fbuf, fsend, frecv, fdec, ucol, bas,
     in_sem, own_sem, csem, lsem, fsem, ring_s, ring_r,
 ):
     y, z = lax.axis_index("y"), lax.axis_index("z")
@@ -78,8 +80,10 @@
         pl.semaphore_signal(barrier, inc=1, device_id=peer, device_id_type=MESH_ID)
     cf_in = pltpu.make_async_copy(cf_hbm, cf, in_sem.at[0])
     leg_in = pltpu.make_async_copy(leg_hbm, leg, in_sem.at[1])
+    pw_in = pltpu.make_async_copy(pw_hbm, pw, in_sem.at[2])
     cf_in.start()
     leg_in.start()
+    pw_in.start()
 
     def slot_tile(ref, row, j):
         count = min(8, SLOTS - 8 * j)
@@ -92,13 +96,14 @@
     for r in range(12):
         for g in range(2):
             tiles = [slot_tile(cf, r, 3 * g + k) for k in range(3)]
-            at = 8 * (8 * r + 4 * g)
+            at = 8 * (48 * g + 4 * r)
             for k in range(3):
                 cbuf[at + 8 * k : at + 8 * k + 8, :] = tiles[k][:, :128]
             rest = [t[:, 128:] for t in tiles] + [jnp.zeros((8, 8), F32)]
             cbuf[at + 24 : at + 32, :] = jnp.concatenate(rest, 1)
-    for d in range(N):
-        csend[d] = cbuf[pl.ds(d, 96, stride=8), :].astype(BF)
+    for g in range(2):
+        for d in range(N):
+            csend[g, d] = cbuf[pl.ds(384 * g + d, 48, stride=8), :].astype(BF)
     leg_in.wait()
     for i in range(LAT):
         for j in range(PER):
@@ -109,26 +114,17 @@
 
     pl.semaphore_wait(barrier, len(peers))
 
-    own_c = pltpu.make_async_copy(csend.at[z], crecv.at[z], own_sem.at[0])
+    own_c = pltpu.make_async_copy(csend.at[:, z], crecv.at[:, z], own_sem.at[0])
     own_c.start()
-    for t in FAR_FIRST:
-        to = (z + t) % N
-        pltpu.make_async_remote_copy(
-            csend.at[to], crecv.at[z], csem.at[0], csem.at[1], device_id=device(y, to, m), device_id_type=MESH_ID
-        ).start()
-
-    def send_leg(to):
-        pltpu.make_async_remote_copy(
-            lsend.at[to], lrecv.at[z], lsem.at[0], lsem.at[1], device_id=device(y, to, m), device_id_type=MESH_ID
-        ).start()
-
-    for n, t in enumerate(FAR_FIRST + (0,)):
-        to = (z + t) % N
-        for l in range(6):
-            lsend[to, :, 128 * l : 128 * l + 128] = lbuf[l, pl.ds(to, 60, stride=8), :].astype(BF)
-        if n >= 1:
-            send_leg((z + FAR_FIRST[n - 1]) % N)
-    own_l = pltpu.make_async_copy(lsend.at[z], lrecv.at[z], own_sem.at[1])
+    for g in range(2):
+        for t in FAR_FIRST:
+            to = (z + t) % N
+            pltpu.make_async_remote_copy(
+                csend.at[g, to], crecv.at[g, z], csem.at[0, g], csem.at[1, g],
+                device_id=device(y, to, m), device_id_type=MESH_ID,
+            ).start()
+
+    pw_in.wait()
 
     @pl.loop(0, PER * N)
     def _(tile):
@@ -136,7 +132,6 @@
         rows = [jnp.full((1, 128), pw[jnp.minimum(first + d, 359)].astype(F32)) for d in range(8)]
         ucol[pl.ds(pl.multiple_of(tile * 8, 8), 8), :] = jnp.concatenate(rows, 0)
 
-    own_l.start()
     lane = lax.broadcasted_iota(jnp.int32, (16, 128), 1).astype(F32)
 
     def make_basis(first, last):
@@ -156,17 +151,26 @@
                         bas[h, 0, pl.ds(to, 16), 128 * l : 128 * l + 128] = high
                         bas[h, 1, pl.ds(to, 16), 128 * l : 128 * l + 128] = low
 
-    make_basis(0, 8)
+    make_basis(0, EARLY)
+
+    def send_leg(to):
+        pltpu.make_async_remote_copy(
+            lsend.at[to], lrecv.at[z], lsem.at[0], lsem.at[1], device_id=device(y, to, m), device_id_type=MESH_ID
+        ).start()
+
+    for n, t in enumerate(FAR_FIRST + (0,)):
+        to = (z + t) % N
+        for l in range(6):
+            lsend[to, :, 128 * l : 128 * l + 128] = lbuf[l, pl.ds(to, 60, stride=8), :].astype(BF)
+        if n >= 1:
+            send_leg((z + FAR_FIRST[n - 1]) % N)
+    own_l = pltpu.make_async_copy(lsend.at[z], lrecv.at[z], own_sem.at[1])
+
+    own_l.start()
+    make_basis(EARLY, 24)
 
     def wait_bytes(ref, sem):
         pltpu.make_async_copy(ref, ref, sem).wait()
-
-    own_c.wait()
-    wait_bytes(crecv.at[pl.ds(0, 7)], csem.at[1])
-    for s in range(N):
-        cbuf[96 * s : 96 * s + 96, :] = crecv[s].astype(F32)
-    for blk in range(8):
-        gat[y, blk] = cbuf[pl.ds(blk, 96, stride=8), :].astype(BF)
 
     def ring(way, step, half):
         origin = (y - step + N) % N if way == 0 else (y + step) % N
@@ -177,21 +181,21 @@
             device_id=device(to, z, m), device_id_type=MESH_ID,
         )
 
+    own_c.wait()
     for half in range(2):
+        wait_bytes(crecv.at[half, pl.ds(0, 7)], csem.at[1, half])
+        for s in range(N):
+            cbuf[48 * s : 48 * s + 48, :] = crecv[half, s].astype(F32)
+        for blk in range(4):
+            gat[y, 4 * half + blk] = cbuf[pl.ds(blk, 96, stride=4), :].astype(BF)
         for way in range(2):
             ring(way, 0, half).start()
-    done = 8
     for step in range(1, 4):
         for half in range(2):
-            if done < 24:
-                make_basis(done, min(done + 3, 24))
-                done = min(done + 3, 24)
             for way in range(2):
                 if step < 3 or way == half:
                     ring(way, step - 1, half).wait_recv()
                     ring(way, step, half).start()
-    if done < 24:
-        make_basis(done, 24)
     own_l.wait()
     wait_bytes(lrecv.at[pl.ds(0, 7)], lsem.at[1])
     for s in range(N):
@@ -228,7 +232,7 @@
             )
             for e, value in enumerate((first, imag)):
                 at = (12 * h + 6 * e + j) * STRIDE
-                fbuf[at : at + 80, :] = value
+                fbuf[at : at + 80, :] = jnp.where(lane80 < CH, value, 0.0)
 
     lane24 = lax.broadcasted_iota(jnp.int32, (24, 128), 1)
 
@@ -237,17 +241,20 @@
         for i in range(LAT):
             at = 8 * to + i if i < 8 else 64 + 8 * (i - 8) + to
             lats.append(fbuf[pl.ds(at, 24, stride=STRIDE), :])
+        most = jnp.abs(lats[0])
+        for value in lats[1:]:
+            most = jnp.maximum(most, jnp.abs(value))
+        most = jnp.max(most, axis=1, keepdims=True)
+        level = jnp.ceil(jnp.log2(jnp.maximum(most, 1e-30)))
+        gain = jnp.exp2(15.0 - level) * SHRINK
+        lats = [jnp.round(value * gain) for value in lats]
+        level = jnp.broadcast_to(level, (24, 128))
         for k in range(N):
             i, skip = k + k // 4, 21 * (k % 4)
-            keep = CH - skip
-            first = pltpu.roll(lats[i], 128 - skip, axis=1) if skip else lats[i]
-            window = jnp.where(lane24 < keep, first, pltpu.roll(lats[i + 1], keep, axis=1))
-            window = jnp.where(lane24 < ROWS, window, 0.0)
-            most = jnp.max(jnp.abs(window), axis=1, keepdims=True)
-            level = jnp.ceil(jnp.log2(jnp.maximum(most, 1e-30)))
-            scaled = jnp.clip(jnp.round(window * jnp.exp2(15.0 - level)), -32767.0, 32767.0)
-            coded = jnp.where(lane24 < ROWS, scaled, jnp.broadcast_to(level, (24, 128)))
-            fsend[to, k] = coded.astype(jnp.int32).astype(jnp.int16)
+            inside = (lane24 >= skip) & (lane24 < CH)
+            window = jnp.where(inside, lats[i], pltpu.roll(lats[i + 1], CH, axis=1))
+            window = jnp.where(lane24 == (skip + 127) % 128, level, window)
+            fsend[to, k] = window.astype(jnp.int32).astype(jnp.int16)
 
     def send_f(to):
         for t in range(N):
@@ -270,7 +277,8 @@
     own_f = pltpu.make_async_copy(fsend.at[z, m], frecv.at[m * N + z], own_sem.at[2])
     own_f.start()
 
-    wait_bytes(csend.at[pl.ds(0, 7)], csem.at[0])
+    for g in range(2):
+        wait_bytes(csend.at[g, pl.ds(0, 7)], csem.at[0, g])
     wait_bytes(lsend.at[pl.ds(0, 7)], lsem.at[0])
     for way in range(2):
         for step in range(4):
@@ -280,18 +288,19 @@
     own_f.wait()
     wait_bytes(frecv.at[pl.ds(0, 63)], fsem.at[1])
 
-    lane192 = lax.broadcasted_iota(jnp.int32, (192, 128), 1)
+    turn = lax.rem(128 - 21 * lax.rem(m, 4), 128)
 
     @pl.loop(0, 8)
     def _(part):
         coded = frecv[pl.ds(part * 8, 8)].astype(jnp.int32).astype(F32).reshape(192, 128)
-        scale = jnp.exp2(coded[:, 127:128] - 15.0)
-        fdec[pl.ds(pl.multiple_of(part * 192, 8), 192), :] = jnp.where(lane192 < ROWS, coded * scale, 0.0)
+        fdec[pl.ds(pl.multiple_of(part * 192, 8), 192), :] = pltpu.roll(coded, turn, axis=1)
 
     lhs = []
     for h in range(2):
         rows = jnp.concatenate([fdec[pl.ds(12 * h + t, 64, stride=24), :] for t in range(12)], 0)
-        high, low = split_bf16(jnp.transpose(rows))
+        rows = jnp.transpose(rows)
+        rows = rows * (jnp.exp2(rows[127:128, :] - 15.0) * (1.0 / SHRINK))
+        high, low = split_bf16(rows)
         lhs.append((high, jnp.concatenate([high, low], 0)))
     for l in range(3):
         at = slice(256 * l, 256 * l + 256)
@@ -314,17 +323,18 @@
         kernel,
         out_shape=jax.ShapeDtypeStruct((ROWS, LON), F32),
         in_specs=[
-            pl.BlockSpec(memory_space=pltpu.SMEM),
-            pl.BlockSpec(memory_space=pl.ANY),
-            pl.BlockSpec(memory_space=pl.ANY),
+            pl.BlockSpec(memory_space=pltpu.HBM),
+            pl.BlockSpec(memory_space=pltpu.HBM),
+            pl.BlockSpec(memory_space=pltpu.HBM),
         ],
         out_specs=pl.BlockSpec(memory_space=pltpu.VMEM),
         scratch_shapes=[
+            pltpu.SMEM((360,), jnp.int32),
             pltpu.VMEM((LAT, SLOTS, RR), BF),
             pltpu.VMEM((12, SLOTS, 2 * CH), BF),
             pltpu.VMEM((768, 128), F32),
-            pltpu.VMEM((N, 96, 128), BF),
-            pltpu.VMEM((N, 96, 128), BF),
+            pltpu.VMEM((2, N, 48, 128), BF),
+            pltpu.VMEM((2, N, 48, 128), BF),
             pltpu.VMEM((N, 8, 96, 128), BF),
             pltpu.VMEM((6, 480, 128), F32),
             pltpu.VMEM((N, 60, RR), BF),
@@ -336,15 +346,15 @@
             pltpu.VMEM((N * N * 24, 128), F32),
             pltpu.VMEM((384, 128), F32),
             pltpu.VMEM((2, 2, RR, RR), BF),
-            pltpu.SemaphoreType.DMA((2,)),
             pltpu.SemaphoreType.DMA((3,)),
-            pltpu.SemaphoreType.DMA((2,)),
+            pltpu.SemaphoreType.DMA((3,)),
+            pltpu.SemaphoreType.DMA((2, 2)),
             pltpu.SemaphoreType.DMA((2,)),
             pltpu.SemaphoreType.DMA((2,)),
             pltpu.SemaphoreType.DMA((2, 4, 2)),
             pltpu.SemaphoreType.DMA((2, 4, 2)),
         ],
-        compiler_params=pltpu.CompilerParams(collective_id=0, has_side_effects=True, vmem_limit_bytes=40 << 20),
+        compiler_params=pltpu.CompilerParams(collective_id=0, has_side_effects=True, vmem_limit_bytes=67043328),
     )(pair_wave, jnp.transpose(legendre, (1, 0, 2)), jnp.transpose(coefs, (1, 0, 2)))
 
 

time: 62 us -> 57.6 us (0.929)
  Pallas kernels: 58.2 us -> 55.4 us
  local copies, waits for them, and re-layouts: 3.61 us -> 2 us
    pallas_call x1, Pallas kernels: 58.2 us -> 55.4 us  [body(): pl.pallas_call(kernel, out_shape=jax.ShapeDtypeStruct((ROWS, LON), F32),...]
    unnamed x7 -> x1, local copies, waits for them, and re-layouts: 3.61 us -> 2 us
where the time goes in v2:
time: 57.6 us; the launch traced here: 57.4 us
  Pallas kernels  55.4 us (96%)
  local copies, waits for them, and re-layouts  2 us (3%)
    pallas_call x1, Pallas kernels, body(): pl.pallas_call(kernel, out_shape=jax.ShapeDtypeStruct((ROWS, LON), F32),...  55.4 us
    unnamed x1, local copies, waits for them, and re-layouts  2 us

profile of v2, /device:TPU:1, one launch (start us, length us, event | category | flops | bytes accessed | tf_op | source)
XLA Modules:
  0.0 57.4 jit_solution(12268282431785072403)
XLA Ops:
  0.0 55.4 %shard_map.37 = f32[105,1440]{1,0:T(8,128)} custom-call(s32[360]{0:T(512)} %pw_hbm.1, bf16[10,45,768]{2,1,0:T(8,128)(2,1)} %bitcast.2, bf16[12,45,168]{2,1,0:T(8,128)(2,1)} %bitcast.3), custom_call_target="tpu_custom_call" | custom-call | tf_op jit(solution)/shard_map/pallas_call | solution.py:322
  55.4 2.0 %copy.5 = f32[105,1440]{1,0:T(8,128)} copy(f32[105,1440]{1,0:T(8,128)} %shard_map.37) | data formatting | bytes 1209600

commit v3 on v2

v3 whole, which is shorter than its diff:
```python
import math

import jax
import jax.numpy as jnp
import numpy as np
from jax import lax
from jax.experimental import pallas as pl
from jax.experimental.pallas import tpu as pltpu
from jax.sharding import Mesh
from jax.sharding import PartitionSpec as P

DEG = 720
LON = 1440
HALF = LON // 2
CH = 84
LAT = 10
SLOTS = 45
PER = 6
N = 8
ROWS = 105
RR = 768
F32 = jnp.float32
BF = jnp.bfloat16
MESH_ID = pl.DeviceIdType.MESH
FAR_FIRST = (4, 3, 5, 2, 6, 1, 7)
STRIDE = 88
BEFORE = (4, 3, 5)
BETWEEN = ((2, 6), (1, 7), ())
EARLY = 8
LATER = 8
SHRINK = 0.9999


def half_angle_fit():
    t = np.cos(np.linspace(0, np.pi, 4001)) * (np.pi / 2)
    sin_c = np.linalg.lstsq(np.stack([t ** (2 * i + 1) for i in range(5)], 1), np.sin(t), rcond=None)[0]
    cos_c = np.linalg.lstsq(np.stack([t ** (2 * i) for i in range(6)], 1), np.cos(t), rcond=None)[0]
    return [float(v) for v in sin_c], [float(v) for v in cos_c]


SIN_C, COS_C = half_angle_fit()


def horner(coefs, square):
    total = jnp.full_like(square, coefs[-1])
    for value in coefs[-2::-1]:
        total = total * square + value
    return total


def wave_rows(waves, weight, lon_at):
    product = waves * lon_at
    turns = jnp.round(product * (1.0 / LON))
    half = (product - turns * float(LON)) * (math.pi / LON)
    square = half * half
    sine = half * horner(SIN_C, square)
    cosine = horner(COS_C, square)
    twice = (2.0 * weight) * sine
    return weight - twice * sine, -twice * cosine


def split_bf16(x):
    high = x.astype(BF)
    return high, (x - high.astype(F32)).astype(BF)


def natural_rows():
    lane = lax.broadcasted_iota(jnp.int32, (1, RR), 1).astype(F32)
    z_at = jnp.floor((lane + 0.5) * (1.0 / 96))
    rest = lane - 96.0 * z_at
    y_at = jnp.floor((rest + 0.5) * (1.0 / 12))
    return lane, (8.0 * y_at + z_at) * 12.0 + rest - 12.0 * y_at


def kernel(
    pw_hbm, leg_hbm, cf_hbm, out,
    pw, leg, cf, perm, cbuf, csend, crecv, gat, lbuf, lsend, lrecv, ltail, fbuf, fsend, frecv, fdec, ucol, bas,
    in_sem, own_sem, csem, lsem, fsem, ring_s, ring_r,
):
    y, z = lax.axis_index("y"), lax.axis_index("z")
    m = 2 * lax.axis_index("x") + lax.axis_index("c")
    along, across = (z, y), (y, z)

    def device(kind, along_at, across_at, m_at):
        place = (across_at, along_at) if kind == 0 else (along_at, across_at)
        return (*place, m_at // 2, m_at % 2)

    barrier = pltpu.get_barrier_semaphore()
    peers = [device(kind, (along[kind] + t) % N, across[kind], m) for t in FAR_FIRST for kind in range(2)]
    peers += [device(0, z, y, (m + t) % N) for t in FAR_FIRST]
    for peer in peers:
        pl.semaphore_signal(barrier, inc=1, device_id=peer, device_id_type=MESH_ID)
    cf_in = pltpu.make_async_copy(cf_hbm, cf, in_sem.at[0])
    leg_in = pltpu.make_async_copy(leg_hbm, leg, in_sem.at[1])
    pw_in = pltpu.make_async_copy(pw_hbm, pw, in_sem.at[2])
    cf_in.start()
    leg_in.start()
    pw_in.start()

    lane_row, natural = natural_rows()

    @pl.loop(0, 48)
    def _(block):
        row = lax.broadcasted_iota(jnp.int32, (16, RR), 0).astype(F32) + (16 * block).astype(F32)
        perm[pl.ds(pl.multiple_of(block * 16, 16), 16), :] = jnp.where(row == natural, 1.0, 0.0).astype(BF)

    def slot_tile(ref, row, j):
        count = min(8, SLOTS - 8 * j)
        tile = ref[row, 8 * j : 8 * j + count, :].astype(F32)
        if count < 8:
            tile = jnp.concatenate([tile, jnp.zeros((8 - count, tile.shape[1]), F32)], 0)
        return tile

    cf_in.wait()
    for r in range(12):
        for g in range(2):
            tiles = [slot_tile(cf, r, 3 * g + k) for k in range(3)]
            at = 8 * (48 * g + 4 * r)
            for k in range(3):
                cbuf[at + 8 * k : at + 8 * k + 8, :] = tiles[k][:, :128]
            rest = [t[:, 128:] for t in tiles] + [jnp.zeros((8, 8), F32)]
            cbuf[at + 24 : at + 32, :] = jnp.concatenate(rest, 1)
    for g in range(2):
        for d in range(N):
            csend[g, d] = cbuf[pl.ds(384 * g + d, 48, stride=8), :].astype(BF)

    def put_leg(kind, i, k, tile):
        at = 240 * kind + 8 * (8 * k + i if i < 8 else 24 + 2 * k + i - 8)
        for l in range(6):
            lbuf[l, at : at + 8, :] = tile[:, 128 * l : 128 * l + 128]

    def pack_leg(kind):
        for d in range(N):
            for l in range(6):
                rows = lbuf[l, pl.ds(240 * kind + d, 30, stride=8), :]
                lsend[kind, d, :, 128 * l : 128 * l + 128] = rows.astype(BF)

    leg_in.wait()
    for i in range(LAT):
        for k in range(3):
            put_leg(0, i, k, slot_tile(leg, i, k))
    pack_leg(0)

    pl.semaphore_wait(barrier, len(peers))

    own_c = pltpu.make_async_copy(
        csend.at[0, along[0]], crecv.at[0, along[0]], own_sem.at[0]
    ), pltpu.make_async_copy(csend.at[1, along[1]], crecv.at[1, along[1]], own_sem.at[1])
    for t in FAR_FIRST:
        for kind in range(2):
            to = (along[kind] + t) % N
            pltpu.make_async_remote_copy(
                csend.at[kind, to], crecv.at[kind, along[kind]], csem.at[0, kind], csem.at[1, kind],
                device_id=device(kind, to, across[kind], m), device_id_type=MESH_ID,
            ).start()
    own_c[0].start()
    own_c[1].start()

    def send_leg(t):
        for kind in range(2):
            to = (along[kind] + t) % N
            pltpu.make_async_remote_copy(
                lsend.at[kind, to], lrecv.at[kind, t], lsem.at[0, kind], lsem.at[1, kind],
                device_id=device(kind, to, across[kind], m), device_id_type=MESH_ID,
            ).start()

    rows = [jnp.concatenate([slot_tile(leg, i, 3 + k) for k in range(3)], 0).astype(BF) for i in range(LAT)]
    moved = jnp.dot(jnp.concatenate(rows, 0), perm[...], preferred_element_type=F32)
    for i in range(LAT):
        for k in range(3):
            put_leg(1, i, k, moved[24 * i + 8 * k : 24 * i + 8 * k + 8])
    pack_leg(1)
    pw_in.wait()

    @pl.loop(0, PER * N)
    def _(tile):
        first = SLOTS * (tile % N) + 8 * (tile // N)
        rows = [jnp.full((1, 128), pw[jnp.minimum(first + d, 359)].astype(F32)) for d in range(8)]
        ucol[pl.ds(pl.multiple_of(tile * 8, 8), 8), :] = jnp.concatenate(rows, 0)

    lane = lax.broadcasted_iota(jnp.int32, (16, 128), 1).astype(F32)

    def make_basis(first, last):
        @pl.loop(first, last)
        def _(block):
            at = pl.multiple_of(block * 16, 16)
            u = ucol[pl.ds(at, 16), :]
            odd = u - 2.0 * jnp.floor(u * 0.5) > 0.5
            even_wave = jnp.where(odd, float(DEG - 1) - u, u)
            weight = jnp.where(even_wave == 0.0, 1.0, 2.0)
            for h, (wave, wt) in enumerate(((even_wave, weight), (float(DEG - 1) - even_wave, 2.0))):
                for l in range(6):
                    pair = wave_rows(wave, wt, lane + 128.0 * l)
                    for e in range(2):
                        high, low = split_bf16(pair[e])
                        to = pl.multiple_of(384 * e + at, 16)
                        bas[h, 0, pl.ds(to, 16), 128 * l : 128 * l + 128] = high
                        bas[h, 1, pl.ds(to, 16), 128 * l : 128 * l + 128] = low

    own_l = [
        pltpu.make_async_copy(lsend.at[kind, along[kind]], lrecv.at[kind, 0], own_sem.at[2 + kind])
        for kind in range(2)
    ]
    for t in BEFORE:
        send_leg(t)
    own_l[0].start()
    own_l[1].start()
    make_basis(0, EARLY)

    def wait_bytes(ref, sem):
        pltpu.make_async_copy(ref, ref, sem).wait()

    def ring(kind, way, step, half):
        own = across[kind]
        origin = (own - step + N) % N if way == 0 else (own + step) % N
        part = gat.at[kind, origin, pl.ds(2 * half, 2)]
        to = (own + 1) % N if way == 0 else (own + N - 1) % N
        return pltpu.make_async_remote_copy(
            part, part, ring_s.at[kind, way, step, half], ring_r.at[kind, way, step, half],
            device_id=device(kind, along[kind], to, m), device_id_type=MESH_ID,
        )

    for kind in range(2):
        own_c[kind].wait()
        wait_bytes(crecv.at[kind, pl.ds(0, 7)], csem.at[1, kind])
        for s in range(N):
            cbuf[48 * s : 48 * s + 48, :] = crecv[kind, s].astype(F32)
        for blk in range(4):
            gat[kind, across[kind], blk] = cbuf[pl.ds(blk, 96, stride=4), :].astype(BF)
        for half in range(2):
            for way in range(2):
                ring(kind, way, 0, half).start()
    for step in range(1, 4):
        for t in BETWEEN[step - 1]:
            send_leg(t)
        if step < 3:
            make_basis(EARLY + LATER * (step - 1), min(24, EARLY + LATER * step))
        for half in range(2):
            for kind in range(2):
                for way in range(2):
                    if step < 3 or way == half:
                        ring(kind, way, step - 1, half).wait_recv()
                        ring(kind, way, step, half).start()
    for kind in range(2):
        own_l[kind].wait()
        wait_bytes(lrecv.at[kind, pl.ds(0, 7)], lsem.at[1, kind])
        for t in range(N):
            for l in range(6):
                ltail[kind, l, 8 * t : 8 * t + 6, :] = lrecv[kind, t, 24:30, 128 * l : 128 * l + 128].astype(F32)
    for kind in range(2):
        ring(kind, 0, 2, 1).wait_recv()
        ring(kind, 1, 2, 0).wait_recv()
        ring(kind, 0, 3, 0).wait_recv()
        ring(kind, 1, 3, 1).wait_recv()

    lane80 = lax.broadcasted_iota(jnp.int32, (80, 128), 1)
    for j in range(PER):
        kind, k = divmod(j, 3)
        u = pw[SLOTS * m + jnp.minimum(8 * j + along[kind], SLOTS - 1)]
        row_at = natural if kind else lane_row
        low = (row_at < (DEG - u).astype(F32)).astype(F32)
        high = (row_at <= float(DEG)).astype(F32) - low
        swap = lax.rem(u, 2).astype(F32)
        masks = [(low + swap * (high - low)).astype(BF), (high + swap * (low - high)).astype(BF)]
        main = lrecv[kind, :, 8 * k : 8 * k + 8, :].reshape(64, RR)
        tail = [[ltail[kind, l, pl.ds(2 * k + n, 8, stride=8), :] for l in range(6)] for n in range(2)]
        tail = jnp.concatenate([jnp.concatenate(t, 1) for t in tail], 0)
        table = jnp.concatenate([main, tail.astype(BF)], 0)
        lhs = jnp.concatenate([table * masks[0], table * masks[1]], 0)
        rhs = jnp.concatenate([gat[kind, :, k].reshape(RR, 128), gat[kind, :, 3].reshape(RR, 128)], 1)
        sums = jnp.dot(lhs, rhs, preferred_element_type=F32)
        for h in range(2):
            first = sums[80 * h : 80 * h + 80, :128]
            second = sums[80 * h : 80 * h + 80, 128:]
            imag = jnp.where(
                lane80 < 44, pltpu.roll(first, 44, axis=1), pltpu.roll(second, (44 - 40 * k) % 128, axis=1)
            )
            for e, value in enumerate((first, imag)):
                n = 6 * h + 3 * e + k
                at = (8 * kind + n if n < 8 else 16 + 4 * kind + n - 8) * STRIDE
                fbuf[at : at + 80, :] = jnp.where(lane80 < CH, value, 0.0)

    lane24 = lax.broadcasted_iota(jnp.int32, (24, 128), 1)

    def pack(t):
        lats = []
        for i in range(LAT):
            at = 8 * t + i if i < 8 else 64 + 8 * (i - 8) + t
            lats.append(fbuf[pl.ds(at, 24, stride=STRIDE), :])
        most = jnp.abs(lats[0])
        for value in lats[1:]:
            most = jnp.maximum(most, jnp.abs(value))
        most = jnp.max(most, axis=1, keepdims=True)
        level = jnp.ceil(jnp.log2(jnp.maximum(most, 1e-30)))
        gain = jnp.exp2(15.0 - level) * SHRINK
        lats = [jnp.round(value * gain) for value in lats]
        level = jnp.broadcast_to(level, (24, 128))
        for k in range(N):
            i, skip = k + k // 4, 21 * (k % 4)
            inside = (lane24 >= skip) & (lane24 < CH)
            window = jnp.where(inside, lats[i], pltpu.roll(lats[i + 1], CH, axis=1))
            window = jnp.where(lane24 == (skip + 127) % 128, level, window).astype(jnp.int32)
            for kind in range(2):
                fsend[t, k, kind, 0:8] = window[8 * kind : 8 * kind + 8].astype(jnp.int16)
                fsend[t, k, kind, 8:12] = window[16 + 4 * kind : 20 + 4 * kind].astype(jnp.int16)

    def send_f(t):
        for n in range(0 if t else 1, N):
            m_to = (m + n) % N
            for kind in range(2):
                to = (along[kind] - t + N) % N
                pltpu.make_async_remote_copy(
                    fsend.at[t, m_to, kind], frecv.at[kind, m * N + along[kind]], fsem.at[0, kind], fsem.at[1, kind],
                    device_id=device(kind, to, across[kind], m_to), device_id_type=MESH_ID,
                ).start()

    order = FAR_FIRST + (0,)
    for n, t in enumerate(order):
        pack(t)
        if n >= 1:
            send_f(order[n - 1])
    send_f(0)
    own_f = [
        pltpu.make_async_copy(fsend.at[0, m, kind], frecv.at[kind, m * N + along[kind]], own_sem.at[4 + kind])
        for kind in range(2)
    ]
    own_f[0].start()
    own_f[1].start()

    for kind in range(2):
        wait_bytes(csend.at[kind, pl.ds(0, 7)], csem.at[0, kind])
        wait_bytes(lsend.at[kind, pl.ds(0, 7)], lsem.at[0, kind])
        for way in range(2):
            for step in range(4):
                for half in range(2):
                    if step < 3 or way == half:
                        ring(kind, way, step, half).wait_send()

    turn = lax.rem(128 - 21 * lax.rem(m, 4), 128)
    for kind in range(2):
        own_f[kind].wait()
        wait_bytes(frecv.at[kind, pl.ds(0, 63)], fsem.at[1, kind])

        @pl.loop(0, 8)
        def _(part):
            coded = frecv[kind, pl.ds(part * 8, 8)].astype(jnp.int32).astype(F32)
            for n in range(8):
                at = pl.multiple_of((64 * kind + part * 8 + n) * 24, 8)
                fdec[pl.ds(at, 12), :] = pltpu.roll(coded[n], turn, axis=1)

    lhs = []
    for h in range(2):
        at = [1536 * kind + 6 * h + 3 * e + k for e in range(2) for kind in range(2) for k in range(3)]
        rows = jnp.concatenate([fdec[pl.ds(first, 64, stride=24), :] for first in at], 0)
        rows = jnp.transpose(rows)
        rows = rows * (jnp.exp2(rows[127:128, :] - 15.0) * (1.0 / SHRINK))
        high, low = split_bf16(rows)
        lhs.append((high, jnp.concatenate([high, low], 0)))
    for l in range(3):
        at = slice(256 * l, 256 * l + 256)
        part = []
        for h in range(2):
            high, both = lhs[h]
            wide = jnp.dot(both, bas[h, 0, :, at], preferred_element_type=F32)
            part.append(
                wide[:128] + wide[128:] + jnp.dot(high, bas[h, 1, :, at], preferred_element_type=F32)
            )
        count = min(256, HALF - 256 * l)
        out[:, 256 * l : 256 * l + count] = (part[0] + part[1])[:ROWS, :count]
        out[:, HALF + 256 * l : HALF + 256 * l + count] = (part[0] - part[1])[:ROWS, :count]
    for kind in range(2):
        wait_bytes(frecv.at[kind, pl.ds(0, 63)], fsem.at[0, kind])


def body(pair_wave, legendre, coefs):
    i16 = jnp.int16
    return pl.pallas_call(
        kernel,
        out_shape=jax.ShapeDtypeStruct((ROWS, LON), F32),
        in_specs=[
            pl.BlockSpec(memory_space=pltpu.HBM),
            pl.BlockSpec(memory_space=pltpu.HBM),
            pl.BlockSpec(memory_space=pltpu.HBM),
        ],
        out_specs=pl.BlockSpec(memory_space=pltpu.VMEM),
        scratch_shapes=[
            pltpu.SMEM((360,), jnp.int32),
            pltpu.VMEM((LAT, SLOTS, RR), BF),
            pltpu.VMEM((12, SLOTS, 2 * CH), BF),
            pltpu.VMEM((RR, RR), BF),
            pltpu.VMEM((768, 128), F32),
            pltpu.VMEM((2, N, 48, 128), BF),
            pltpu.VMEM((2, N, 48, 128), BF),
            pltpu.VMEM((2, N, 4, 96, 128), BF),
            pltpu.VMEM((6, 480, 128), F32),
            pltpu.VMEM((2, N, 30, RR), BF),
            pltpu.VMEM((2, N, 30, RR), BF),
            pltpu.VMEM((2, 6, 64, 128), F32),
            pltpu.VMEM((24 * STRIDE, 128), F32),
            pltpu.VMEM((N, N, 2, 12, 128), i16),
            pltpu.VMEM((2, N * N, 12, 128), i16),
            pltpu.VMEM((2 * N * N * 24, 128), F32),
            pltpu.VMEM((384, 128), F32),
            pltpu.VMEM((2, 2, RR, RR), BF),
            pltpu.SemaphoreType.DMA((3,)),
            pltpu.SemaphoreType.DMA((6,)),
            pltpu.SemaphoreType.DMA((2, 2)),
            pltpu.SemaphoreType.DMA((2, 2)),
            pltpu.SemaphoreType.DMA((2, 2)),
            pltpu.SemaphoreType.DMA((2, 2, 4, 2)),
            pltpu.SemaphoreType.DMA((2, 2, 4, 2)),
        ],
        compiler_params=pltpu.CompilerParams(collective_id=0, has_side_effects=True, vmem_limit_bytes=67043328),
    )(pair_wave, jnp.transpose(legendre, (1, 0, 2)), jnp.transpose(coefs, (1, 0, 2)))


def solution(mesh):
    split = Mesh(mesh.devices.reshape(N, N, 4, 2), ("y", "z", "x", "c"))
    placed = (P(), P(("x", "c"), ("y", "z"), None), P(("x", "c"), ("y", "z"), None))
    return jax.shard_map(
        body, mesh=split, in_specs=placed, out_specs=P(("y", "z", "x", "c"), None), check_vma=False
    )
```

time: 57.6 us -> 54.2 us (0.941)
  Pallas kernels: 55.4 us -> 52 us
    pallas_call x1, Pallas kernels: 55.4 us -> 52 us  [body(): pl.pallas_call(kernel, out_shape=jax.ShapeDtypeStruct((ROWS, LON), F32),...]
where the time goes in v3:
time: 54.2 us; the launch traced here: 54 us
  Pallas kernels  52 us (96%)
  local copies, waits for them, and re-layouts  2 us (4%)
    pallas_call x1, Pallas kernels, body(): pl.pallas_call(kernel, out_shape=jax.ShapeDtypeStruct((ROWS, LON), F32),...  52 us
    unnamed x1, local copies, waits for them, and re-layouts  2 us

profile of v3, /device:TPU:1, one launch (start us, length us, event | category | flops | bytes accessed | tf_op | source)
XLA Modules:
  0.0 54.0 jit_solution(15846429843955683109)
XLA Ops:
  0.0 52.0 %shard_map.37 = f32[105,1440]{1,0:T(8,128)} custom-call(s32[360]{0:T(512)} %pw_hbm.1, bf16[10,45,768]{2,1,0:T(8,128)(2,1)} %bitcast.2, bf16[12,45,168]{2,1,0:T(8,128)(2,1)} %bitcast.3), custom_call_target="tpu_custom_call" | custom-call | tf_op jit(solution)/shard_map/pallas_call | solution.py:377
  52.0 2.0 %copy.5 = f32[105,1440]{1,0:T(8,128)} copy(f32[105,1440]{1,0:T(8,128)} %shard_map.37) | data formatting | bytes 1209600

commit v4 on v3

--- a/solution.py
+++ b/solution.py
@@ -25,7 +25,7 @@
 FAR_FIRST = (4, 3, 5, 2, 6, 1, 7)
 STRIDE = 88
 BEFORE = (4, 3, 5)
-BETWEEN = ((2, 6), (1, 7), ())
+BETWEEN = ((2, 6), (1, 7))
 EARLY = 8
 LATER = 8
 SHRINK = 0.9999
@@ -170,6 +170,8 @@
         for k in range(3):
             put_leg(1, i, k, moved[24 * i + 8 * k : 24 * i + 8 * k + 8])
     pack_leg(1)
+    for t in BEFORE:
+        send_leg(t)
     pw_in.wait()
 
     @pl.loop(0, PER * N)
@@ -201,8 +203,6 @@
         pltpu.make_async_copy(lsend.at[kind, along[kind]], lrecv.at[kind, 0], own_sem.at[2 + kind])
         for kind in range(2)
     ]
-    for t in BEFORE:
-        send_leg(t)
     own_l[0].start()
     own_l[1].start()
     make_basis(0, EARLY)
@@ -211,10 +211,10 @@
         pltpu.make_async_copy(ref, ref, sem).wait()
 
     def ring(kind, way, step, half):
-        own = across[kind]
-        origin = (own - step + N) % N if way == 0 else (own + step) % N
+        own, back, on = across[kind], min(step, 2), 1 + step // 3
+        origin = (own - back + N) % N if way == 0 else (own + back) % N
         part = gat.at[kind, origin, pl.ds(2 * half, 2)]
-        to = (own + 1) % N if way == 0 else (own + N - 1) % N
+        to = (own + on) % N if way == 0 else (own + N - on) % N
         return pltpu.make_async_remote_copy(
             part, part, ring_s.at[kind, way, step, half], ring_r.at[kind, way, step, half],
             device_id=device(kind, along[kind], to, m), device_id_type=MESH_ID,
@@ -230,17 +230,17 @@
         for half in range(2):
             for way in range(2):
                 ring(kind, way, 0, half).start()
-    for step in range(1, 4):
+    for step in range(1, 3):
         for t in BETWEEN[step - 1]:
             send_leg(t)
-        if step < 3:
-            make_basis(EARLY + LATER * (step - 1), min(24, EARLY + LATER * step))
+        make_basis(EARLY + LATER * (step - 1), min(24, EARLY + LATER * step))
         for half in range(2):
             for kind in range(2):
                 for way in range(2):
-                    if step < 3 or way == half:
-                        ring(kind, way, step - 1, half).wait_recv()
-                        ring(kind, way, step, half).start()
+                    ring(kind, way, step - 1, half).wait_recv()
+                    if step == 2 and way == half:
+                        ring(kind, way, 3, half).start()
+                    ring(kind, way, step, half).start()
     for kind in range(2):
         own_l[kind].wait()
         wait_bytes(lrecv.at[kind, pl.ds(0, 7)], lsem.at[1, kind])
@@ -248,10 +248,10 @@
             for l in range(6):
                 ltail[kind, l, 8 * t : 8 * t + 6, :] = lrecv[kind, t, 24:30, 128 * l : 128 * l + 128].astype(F32)
     for kind in range(2):
-        ring(kind, 0, 2, 1).wait_recv()
-        ring(kind, 1, 2, 0).wait_recv()
-        ring(kind, 0, 3, 0).wait_recv()
-        ring(kind, 1, 3, 1).wait_recv()
+        for way in range(2):
+            for half in range(2):
+                ring(kind, way, 2, half).wait_recv()
+            ring(kind, way, 3, way).wait_recv()
 
     lane80 = lax.broadcasted_iota(jnp.int32, (80, 128), 1)
     for j in range(PER):
@@ -310,7 +310,7 @@
             for kind in range(2):
                 to = (along[kind] - t + N) % N
                 pltpu.make_async_remote_copy(
-                    fsend.at[t, m_to, kind], frecv.at[kind, m * N + along[kind]], fsem.at[0, kind], fsem.at[1, kind],
+                    fsend.at[t, m_to, kind], frecv.at[kind, m * N + along[kind]], fsem.at[0, kind], fsem.at[1 + kind, t],
                     device_id=device(kind, to, across[kind], m_to), device_id_type=MESH_ID,
                 ).start()
 
@@ -337,16 +337,16 @@
                         ring(kind, way, step, half).wait_send()
 
     turn = lax.rem(128 - 21 * lax.rem(m, 4), 128)
-    for kind in range(2):
-        own_f[kind].wait()
-        wait_bytes(frecv.at[kind, pl.ds(0, 63)], fsem.at[1, kind])
-
-        @pl.loop(0, 8)
-        def _(part):
-            coded = frecv[kind, pl.ds(part * 8, 8)].astype(jnp.int32).astype(F32)
-            for n in range(8):
-                at = pl.multiple_of((64 * kind + part * 8 + n) * 24, 8)
-                fdec[pl.ds(at, 12), :] = pltpu.roll(coded[n], turn, axis=1)
+    for t in order:
+        for kind in range(2):
+            if t == 0:
+                own_f[kind].wait()
+            wait_bytes(frecv.at[kind, pl.ds(0, 8 if t else 7)], fsem.at[1 + kind, t])
+            source = (along[kind] + t) % N
+            for n in range(N):
+                coded = frecv[kind, 8 * n + source].astype(jnp.int32).astype(F32)
+                at = pl.multiple_of((64 * kind + 8 * n + source) * 24, 8)
+                fdec[pl.ds(at, 12), :] = pltpu.roll(coded, turn, axis=1)
 
     lhs = []
     for h in range(2):
@@ -406,7 +406,7 @@
             pltpu.SemaphoreType.DMA((6,)),
             pltpu.SemaphoreType.DMA((2, 2)),
             pltpu.SemaphoreType.DMA((2, 2)),
-            pltpu.SemaphoreType.DMA((2, 2)),
+            pltpu.SemaphoreType.DMA((3, N)),
             pltpu.SemaphoreType.DMA((2, 2, 4, 2)),
             pltpu.SemaphoreType.DMA((2, 2, 4, 2)),
         ],

time: 54.2 us -> 52 us (0.959)
  Pallas kernels: 52 us -> 49.9 us
    pallas_call x1, Pallas kernels: 52 us -> 49.9 us  [body(): pl.pallas_call(kernel, out_shape=jax.ShapeDtypeStruct((ROWS, LON), F32),...]
where the time goes in v4:
time: 52 us; the launch traced here: 51.9 us
  Pallas kernels  49.9 us (96%)
  local copies, waits for them, and re-layouts  2 us (4%)
    pallas_call x1, Pallas kernels, body(): pl.pallas_call(kernel, out_shape=jax.ShapeDtypeStruct((ROWS, LON), F32),...  49.9 us
    unnamed x1, local copies, waits for them, and re-layouts  2 us

profile of v4, /device:TPU:1, one launch (start us, length us, event | category | flops | bytes accessed | tf_op | source)
XLA Modules:
  0.0 51.9 jit_solution(5079337342028667897)
XLA Ops:
  0.0 49.9 %shard_map.37 = f32[105,1440]{1,0:T(8,128)} custom-call(s32[360]{0:T(512)} %pw_hbm.1, bf16[10,45,768]{2,1,0:T(8,128)(2,1)} %bitcast.2, bf16[12,45,168]{2,1,0:T(8,128)(2,1)} %bitcast.3), custom_call_target="tpu_custom_call" | custom-call | tf_op jit(solution)/shard_map/pallas_call | solution.py:377
  49.9 2.0 %copy.5 = f32[105,1440]{1,0:T(8,128)} copy(f32[105,1440]{1,0:T(8,128)} %shard_map.37) | data formatting | bytes 1209600

commit v5 on v4

--- a/solution.py
+++ b/solution.py
@@ -18,14 +18,15 @@
 PER = 6
 N = 8
 ROWS = 105
+PADDED = 112
 RR = 768
 F32 = jnp.float32
 BF = jnp.bfloat16
 MESH_ID = pl.DeviceIdType.MESH
 FAR_FIRST = (4, 3, 5, 2, 6, 1, 7)
 STRIDE = 88
-BEFORE = (4, 3, 5)
-BETWEEN = ((2, 6), (1, 7))
+BEFORE = (1, 7, 4)
+BETWEEN = ((2, 6), (3, 5))
 EARLY = 8
 LATER = 8
 SHRINK = 0.9999
@@ -282,19 +283,20 @@
 
     lane24 = lax.broadcasted_iota(jnp.int32, (24, 128), 1)
 
+    def lats_of(t):
+        at = [8 * t + i if i < 8 else 64 + 8 * (i - 8) + t for i in range(LAT)]
+        return [fbuf[pl.ds(first, 24, stride=STRIDE), :] for first in at]
+
+    def level_of(t):
+        most = [jnp.abs(value) for value in lats_of(t)]
+        while len(most) > 1:
+            most = [jnp.maximum(a, b) for a, b in zip(most[::2], most[1::2])] + most[len(most) // 2 * 2 :]
+        return jnp.ceil(jnp.log2(jnp.maximum(jnp.max(most[0], axis=1, keepdims=True), 1e-30)))
+
     def pack(t):
-        lats = []
-        for i in range(LAT):
-            at = 8 * t + i if i < 8 else 64 + 8 * (i - 8) + t
-            lats.append(fbuf[pl.ds(at, 24, stride=STRIDE), :])
-        most = jnp.abs(lats[0])
-        for value in lats[1:]:
-            most = jnp.maximum(most, jnp.abs(value))
-        most = jnp.max(most, axis=1, keepdims=True)
-        level = jnp.ceil(jnp.log2(jnp.maximum(most, 1e-30)))
-        gain = jnp.exp2(15.0 - level) * SHRINK
-        lats = [jnp.round(value * gain) for value in lats]
-        level = jnp.broadcast_to(level, (24, 128))
+        gain = jnp.exp2(15.0 - levels[t]) * SHRINK
+        lats = [jnp.round(value * gain) for value in lats_of(t)]
+        level = jnp.broadcast_to(levels[t], (24, 128))
         for k in range(N):
             i, skip = k + k // 4, 21 * (k % 4)
             inside = (lane24 >= skip) & (lane24 < CH)
@@ -315,6 +317,7 @@
                 ).start()
 
     order = FAR_FIRST + (0,)
+    levels = {t: level_of(t) for t in order}
     for n, t in enumerate(order):
         pack(t)
         if n >= 1:
@@ -353,7 +356,7 @@
         at = [1536 * kind + 6 * h + 3 * e + k for e in range(2) for kind in range(2) for k in range(3)]
         rows = jnp.concatenate([fdec[pl.ds(first, 64, stride=24), :] for first in at], 0)
         rows = jnp.transpose(rows)
-        rows = rows * (jnp.exp2(rows[127:128, :] - 15.0) * (1.0 / SHRINK))
+        rows = rows[:PADDED] * (jnp.exp2(rows[127:128, :] - 15.0) * (1.0 / SHRINK))
         high, low = split_bf16(rows)
         lhs.append((high, jnp.concatenate([high, low], 0)))
     for l in range(3):
@@ -363,7 +366,7 @@
             high, both = lhs[h]
             wide = jnp.dot(both, bas[h, 0, :, at], preferred_element_type=F32)
             part.append(
-                wide[:128] + wide[128:] + jnp.dot(high, bas[h, 1, :, at], preferred_element_type=F32)
+                wide[:PADDED] + wide[PADDED:] + jnp.dot(high, bas[h, 1, :, at], preferred_element_type=F32)
             )
         count = min(256, HALF - 256 * l)
         out[:, 256 * l : 256 * l + count] = (part[0] + part[1])[:ROWS, :count]
@@ -376,7 +379,7 @@
     i16 = jnp.int16
     return pl.pallas_call(
         kernel,
-        out_shape=jax.ShapeDtypeStruct((ROWS, LON), F32),
+        out_shape=pltpu.VMEM((ROWS, LON), F32),
         in_specs=[
             pl.BlockSpec(memory_space=pltpu.HBM),
             pl.BlockSpec(memory_space=pltpu.HBM),
@@ -410,7 +413,7 @@
             pltpu.SemaphoreType.DMA((2, 2, 4, 2)),
             pltpu.SemaphoreType.DMA((2, 2, 4, 2)),
         ],
-        compiler_params=pltpu.CompilerParams(collective_id=0, has_side_effects=True, vmem_limit_bytes=67043328),
+        compiler_params=pltpu.CompilerParams(collective_id=0, has_side_effects=True, vmem_limit_bytes=62000000),
     )(pair_wave, jnp.transpose(legendre, (1, 0, 2)), jnp.transpose(coefs, (1, 0, 2)))
 
 

time: 52 us -> 49.9 us (0.960)
  local copies, waits for them, and re-layouts: 2 us -> 0.85 us
  Pallas kernels: 49.9 us -> 48.9 us
    unnamed x1, local copies, waits for them, and re-layouts: 2 us -> 0.85 us
    pallas_call x1, Pallas kernels: 49.9 us -> 48.9 us  [body(): pl.pallas_call(kernel, out_shape=pltpu.VMEM((ROWS, LON), F32), in_specs=[...]
where the time goes in v5:
time: 49.9 us; the launch traced here: 49.7 us
  Pallas kernels  48.9 us (98%)
  local copies, waits for them, and re-layouts  0.85 us (2%)
    pallas_call x1, Pallas kernels, body(): pl.pallas_call(kernel, out_shape=pltpu.VMEM((ROWS, LON), F32), in_specs=[...  48.9 us

profile of v5, /device:TPU:1, one launch (start us, length us, event | category | flops | bytes accessed | tf_op | source)
XLA Modules:
  0.0 49.7 jit_solution(335401887521851639)
XLA Ops:
  0.0 48.9 %shard_map.37 = f32[105,1440]{1,0:T(8,128)S(1)} custom-call(s32[360]{0:T(512)} %pw_hbm.1, bf16[10,45,768]{2,1,0:T(8,128)(2,1)} %bitcast.2, bf16[12,45,168]{2,1,0:T(8,128)(2,1)} %bitcast.3), custom_call_target="tpu_custom_call" | custom-call | tf_op jit(solution)/shard_map/pallas_call | solution.py:380
  48.9 0.8 %copy.5 = f32[105,1440]{1,0:T(8,128)} copy(f32[105,1440]{1,0:T(8,128)S(1)} %shard_map.37) | data formatting | bytes 1209600

commit v6 on v5

--- a/solution.py
+++ b/solution.py
@@ -277,15 +277,14 @@
                 lane80 < 44, pltpu.roll(first, 44, axis=1), pltpu.roll(second, (44 - 40 * k) % 128, axis=1)
             )
             for e, value in enumerate((first, imag)):
-                n = 6 * h + 3 * e + k
-                at = (8 * kind + n if n < 8 else 16 + 4 * kind + n - 8) * STRIDE
+                at = (16 * kind + 8 * h + 3 * e + k) * STRIDE
                 fbuf[at : at + 80, :] = jnp.where(lane80 < CH, value, 0.0)
 
-    lane24 = lax.broadcasted_iota(jnp.int32, (24, 128), 1)
+    lane8 = lax.broadcasted_iota(jnp.int32, (8, 128), 1)
 
     def lats_of(t):
         at = [8 * t + i if i < 8 else 64 + 8 * (i - 8) + t for i in range(LAT)]
-        return [fbuf[pl.ds(first, 24, stride=STRIDE), :] for first in at]
+        return [fbuf[pl.ds(first, 32, stride=STRIDE), :] for first in at]
 
     def level_of(t):
         most = [jnp.abs(value) for value in lats_of(t)]
@@ -293,18 +292,21 @@
             most = [jnp.maximum(a, b) for a, b in zip(most[::2], most[1::2])] + most[len(most) // 2 * 2 :]
         return jnp.ceil(jnp.log2(jnp.maximum(jnp.max(most[0], axis=1, keepdims=True), 1e-30)))
 
+    def words(value):
+        whole = value.astype(jnp.int32)
+        return [(whole[at : at + 8] & 0xFFFF) | (whole[at + 8 : at + 16] << 16) for at in (0, 16)]
+
     def pack(t):
         gain = jnp.exp2(15.0 - levels[t]) * SHRINK
-        lats = [jnp.round(value * gain) for value in lats_of(t)]
-        level = jnp.broadcast_to(levels[t], (24, 128))
+        lats = [words(jnp.round(value * gain)) for value in lats_of(t)]
+        level = words(jnp.broadcast_to(levels[t], (32, 128)))
         for k in range(N):
             i, skip = k + k // 4, 21 * (k % 4)
-            inside = (lane24 >= skip) & (lane24 < CH)
-            window = jnp.where(inside, lats[i], pltpu.roll(lats[i + 1], CH, axis=1))
-            window = jnp.where(lane24 == (skip + 127) % 128, level, window).astype(jnp.int32)
+            inside = (lane8 >= skip) & (lane8 < CH)
             for kind in range(2):
-                fsend[t, k, kind, 0:8] = window[8 * kind : 8 * kind + 8].astype(jnp.int16)
-                fsend[t, k, kind, 8:12] = window[16 + 4 * kind : 20 + 4 * kind].astype(jnp.int16)
+                window = jnp.where(inside, lats[i][kind], pltpu.roll(lats[i + 1][kind], CH, axis=1))
+                window = jnp.where(lane8 == (skip + 127) % 128, level[kind], window)
+                fsend[t, k, kind] = window[:PER]
 
     def send_f(t):
         for n in range(0 if t else 1, N):
@@ -347,14 +349,15 @@
             wait_bytes(frecv.at[kind, pl.ds(0, 8 if t else 7)], fsem.at[1 + kind, t])
             source = (along[kind] + t) % N
             for n in range(N):
-                coded = frecv[kind, 8 * n + source].astype(jnp.int32).astype(F32)
-                at = pl.multiple_of((64 * kind + 8 * n + source) * 24, 8)
-                fdec[pl.ds(at, 12), :] = pltpu.roll(coded, turn, axis=1)
+                coded = pltpu.roll(frecv[kind, 8 * n + source], turn, axis=1)
+                at = pl.multiple_of((64 * kind + 8 * n + source) * 8, 8)
+                fdec[pl.ds(at, PER), :] = ((coded << 16) >> 16).astype(F32)
+                fdec[pl.ds(1024 + at, PER), :] = (coded >> 16).astype(F32)
 
     lhs = []
     for h in range(2):
-        at = [1536 * kind + 6 * h + 3 * e + k for e in range(2) for kind in range(2) for k in range(3)]
-        rows = jnp.concatenate([fdec[pl.ds(first, 64, stride=24), :] for first in at], 0)
+        at = [1024 * h + 512 * kind + 3 * e + k for e in range(2) for kind in range(2) for k in range(3)]
+        rows = jnp.concatenate([fdec[pl.ds(first, 64, stride=8), :] for first in at], 0)
         rows = jnp.transpose(rows)
         rows = rows[:PADDED] * (jnp.exp2(rows[127:128, :] - 15.0) * (1.0 / SHRINK))
         high, low = split_bf16(rows)
@@ -376,7 +379,6 @@
 
 
 def body(pair_wave, legendre, coefs):
-    i16 = jnp.int16
     return pl.pallas_call(
         kernel,
         out_shape=pltpu.VMEM((ROWS, LON), F32),
@@ -399,10 +401,10 @@
             pltpu.VMEM((2, N, 30, RR), BF),
             pltpu.VMEM((2, N, 30, RR), BF),
             pltpu.VMEM((2, 6, 64, 128), F32),
-            pltpu.VMEM((24 * STRIDE, 128), F32),
-            pltpu.VMEM((N, N, 2, 12, 128), i16),
-            pltpu.VMEM((2, N * N, 12, 128), i16),
-            pltpu.VMEM((2 * N * N * 24, 128), F32),
+            pltpu.VMEM((32 * STRIDE, 128), F32),
+            pltpu.VMEM((N, N, 2, PER, 128), jnp.int32),
+            pltpu.VMEM((2, N * N, PER, 128), jnp.int32),
+            pltpu.VMEM((2 * 2 * N * N * 8, 128), F32),
             pltpu.VMEM((384, 128), F32),
             pltpu.VMEM((2, 2, RR, RR), BF),
             pltpu.SemaphoreType.DMA((3,)),

time: 49.9 us -> 48.8 us (0.978)
  Pallas kernels: 48.9 us -> 47.8 us
    pallas_call x1, Pallas kernels: 48.9 us -> 47.8 us  [body(): pl.pallas_call(kernel, out_shape=pltpu.VMEM((ROWS, LON), F32), in_specs=[...]
where the time goes in v6:
time: 48.8 us; the launch traced here: 48.7 us
  Pallas kernels  47.8 us (98%)
  local copies, waits for them, and re-layouts  0.85 us (2%)
    pallas_call x1, Pallas kernels, body(): pl.pallas_call(kernel, out_shape=pltpu.VMEM((ROWS, LON), F32), in_specs=[...  47.8 us

profile of v6, /device:TPU:1, one launch (start us, length us, event | category | flops | bytes accessed | tf_op | source)
XLA Modules:
  0.0 48.7 jit_solution(4898864755023437474)
XLA Ops:
  0.0 47.8 %shard_map.37 = f32[105,1440]{1,0:T(8,128)S(1)} custom-call(s32[360]{0:T(512)} %pw_hbm.1, bf16[10,45,768]{2,1,0:T(8,128)(2,1)} %bitcast.2, bf16[12,45,168]{2,1,0:T(8,128)(2,1)} %bitcast.3), custom_call_target="tpu_custom_call" | custom-call | tf_op jit(solution)/shard_map/pallas_call | solution.py:382
  47.8 0.8 %copy.5 = f32[105,1440]{1,0:T(8,128)} copy(f32[105,1440]{1,0:T(8,128)S(1)} %shard_map.37) | data formatting | bytes 1209600

commit v7 on v6

--- a/solution.py
+++ b/solution.py
@@ -342,10 +342,10 @@
                         ring(kind, way, step, half).wait_send()
 
     turn = lax.rem(128 - 21 * lax.rem(m, 4), 128)
-    for t in order:
-        for kind in range(2):
-            if t == 0:
-                own_f[kind].wait()
+    totals = [[0.0, 0.0] for l in range(3)]
+    for kind in range(2):
+        own_f[kind].wait()
+        for t in order:
             wait_bytes(frecv.at[kind, pl.ds(0, 8 if t else 7)], fsem.at[1 + kind, t])
             source = (along[kind] + t) % N
             for n in range(N):
@@ -353,24 +353,24 @@
                 at = pl.multiple_of((64 * kind + 8 * n + source) * 8, 8)
                 fdec[pl.ds(at, PER), :] = ((coded << 16) >> 16).astype(F32)
                 fdec[pl.ds(1024 + at, PER), :] = (coded >> 16).astype(F32)
-
-    lhs = []
-    for h in range(2):
-        at = [1024 * h + 512 * kind + 3 * e + k for e in range(2) for kind in range(2) for k in range(3)]
-        rows = jnp.concatenate([fdec[pl.ds(first, 64, stride=8), :] for first in at], 0)
-        rows = jnp.transpose(rows)
-        rows = rows[:PADDED] * (jnp.exp2(rows[127:128, :] - 15.0) * (1.0 / SHRINK))
-        high, low = split_bf16(rows)
-        lhs.append((high, jnp.concatenate([high, low], 0)))
+        for h in range(2):
+            at = [1024 * h + 512 * kind + n for n in range(PER)]
+            rows = jnp.concatenate([fdec[pl.ds(first, 64, stride=8), :] for first in at], 0)
+            rows = jnp.transpose(rows)
+            rows = rows[:PADDED] * (jnp.exp2(rows[127:128, :] - 15.0) * (1.0 / SHRINK))
+            high, low = split_bf16(rows)
+            both = jnp.concatenate([high, low], 0)
+            for l in range(3):
+                at = slice(256 * l, 256 * l + 256)
+                base = [
+                    jnp.concatenate([bas[h, n, 384 * e + 192 * kind : 384 * e + 192 * kind + 192, at] for e in range(2)], 0)
+                    for n in range(2)
+                ]
+                wide = jnp.dot(both, base[0], preferred_element_type=F32)
+                part = wide[:PADDED] + wide[PADDED:] + jnp.dot(high, base[1], preferred_element_type=F32)
+                totals[l][h] = totals[l][h] + part
     for l in range(3):
-        at = slice(256 * l, 256 * l + 256)
-        part = []
-        for h in range(2):
-            high, both = lhs[h]
-            wide = jnp.dot(both, bas[h, 0, :, at], preferred_element_type=F32)
-            part.append(
-                wide[:PADDED] + wide[PADDED:] + jnp.dot(high, bas[h, 1, :, at], preferred_element_type=F32)
-            )
+        part = totals[l]
         count = min(256, HALF - 256 * l)
         out[:, 256 * l : 256 * l + count] = (part[0] + part[1])[:ROWS, :count]
         out[:, HALF + 256 * l : HALF + 256 * l + count] = (part[0] - part[1])[:ROWS, :count]

time: 48.8 us -> 49.1 us (level)
  no operation moved by 1% of the time
where the time goes in v7:
time: 49.1 us; the launch traced here: 49 us
  Pallas kernels  48.1 us (98%)
  local copies, waits for them, and re-layouts  0.85 us (2%)
    pallas_call x1, Pallas kernels, body(): pl.pallas_call(kernel, out_shape=pltpu.VMEM((ROWS, LON), F32), in_specs=[...  48.1 us

profile of v7, /device:TPU:1, one launch (start us, length us, event | category | flops | bytes accessed | tf_op | source)
XLA Modules:
  0.0 49.0 jit_solution(16453051532368835450)
XLA Ops:
  0.0 48.1 %shard_map.37 = f32[105,1440]{1,0:T(8,128)S(1)} custom-call(s32[360]{0:T(512)} %pw_hbm.1, bf16[10,45,768]{2,1,0:T(8,128)(2,1)} %bitcast.2, bf16[12,45,168]{2,1,0:T(8,128)(2,1)} %bitcast.3), custom_call_target="tpu_custom_call" | custom-call | tf_op jit(solution)/shard_map/pallas_call | solution.py:382
  48.1 0.8 %copy.5 = f32[105,1440]{1,0:T(8,128)} copy(f32[105,1440]{1,0:T(8,128)S(1)} %shard_map.37) | data formatting | bytes 1209600
